TPU v7x, 32 devices: a whole 2x2x4 slice. The times are simulated.
32 devices in a mesh: grp: 4 (over z), dev: 8 (over y, x, core).
Axes of the slice: x: 2, y: 2, z: 4, core: 2. Of those that a mesh axis runs over, the one named last changes fastest.
Arguments:
- blocks: bfloat16 [4096, 128, 128], P(('grp', 'dev')), may hold values from -0.29882812 to 0.29882812
- ids_one: int32 [2, 4096], P(None, ('grp', 'dev')), may hold values from 0 to 255, as said below
- ids_two: int32 [2, 2048], P(None, ('grp', 'dev')), may hold values from 0 to 127, as said below
- ids_three: int32 [2, 1024], P(None, ('grp', 'dev')), may hold values from 0 to 63
- match_one: int32 [256, 128], replicated, may hold values from 0 to 127, as said below
- match_two: int32 [128, 128], replicated, may hold values from 0 to 127, as said below
- match_three: int32 [64, 128], replicated, may hold values from 0 to 127, as said below
- target_one: int32 [4096], P(('grp', 'dev')), may hold values from 0 to 63
- target_two: int32 [2048], P(('grp', 'dev')), may hold values from 0 to 31
- target_three: int32 [1024], P(('grp', 'dev')), may hold values from 0 to 15
- vertex_weights: float32 [256, 128], P(('grp', 'dev')), may hold values from 0.1 to 120, as said below
Outputs:
- coarse_graph: float32 [512, 128, 128], P(('grp', 'dev'))
- rel_weight: float32 [32, 128], P(('grp', 'dev'))
Inputs may be any that keep to these rules, and one draw needn't show every extreme that they name: `match_one`: rows 2b and 2b + 1 together name every number 0 to 127 exactly twice. `match_two`: rows 2b and 2b + 1 together name every number 0 to 127 exactly twice. `match_three`: rows 2b and 2b + 1 together name every number 0 to 127 exactly twice. `ids_one`: a fine block's row and column vertex blocks, halved by integer division, are the ids_two of the coarse slot it goes to. `ids_two`: a first-level block's row and column vertex blocks, halved by integer division, are the ids_three of the coarse slot it goes to. `vertex_weights`: positive.
All inputs are finite; a program needn't handle non-finite values.
Results may differ from a plain program's by a relative error of at most 0.0003.
Values may be sent and summed in bfloat16 or wider, within the bound.
A program may use at most 128 MiB of HBM per device.

v0:
```python
import functools
import math

import jax
import jax.numpy as jnp
from jax import lax
from jax.experimental import pallas as pl
from jax.experimental.pallas import tpu as pltpu
from jax.sharding import PartitionSpec as P

LEVELS = 32767.0
TINY = 1e-30
NT = (((1,), (1,)), ((), ()))


def hot(row, width):
    names = lax.broadcasted_iota(jnp.int32, (width, width), 0)
    return (names == row).astype(jnp.bfloat16)


def halves(x):
    high = x.astype(jnp.bfloat16)
    low = (x - high.astype(jnp.float32)).astype(jnp.bfloat16)
    return high, low


def columns(halfway, col):
    width = col.shape[1]
    right = hot(col, width)
    left = jnp.concatenate(halves(halfway), axis=1)
    both = jnp.concatenate([right, right], axis=1)
    return lax.dot_general(left, both, NT, preferred_element_type=jnp.float32)


def project_narrow(block, row, col):
    left = hot(row, row.shape[1])
    return columns(jnp.dot(left, block, preferred_element_type=jnp.float32), col)


def project_wide(block, row, col):
    left = hot(row, row.shape[1])
    both = jnp.concatenate([left, left], axis=1)
    stacked = jnp.concatenate(halves(block), axis=0)
    return columns(jnp.dot(both, stacked, preferred_element_type=jnp.float32), col)


def encode(part):
    peak = jnp.maximum(jnp.max(jnp.abs(part), axis=0, keepdims=True), TINY)
    code = jnp.round(part * (LEVELS / peak)).astype(jnp.int32)
    return code.astype(jnp.int16), peak * (1.0 / LEVELS)


def decode(code, scale):
    return code.astype(jnp.int32).astype(jnp.float32) * scale


def fold(weights, row):
    width = row.shape[1]
    right = hot(row, width)
    rest = jnp.broadcast_to(weights, (8, width))
    total = jnp.zeros((8, width), jnp.float32)
    for _ in range(3):
        part = rest.astype(jnp.bfloat16)
        rest = rest - part.astype(jnp.float32)
        total = total + lax.dot_general(part, right, NT, preferred_element_type=jnp.float32)
    return total[:1]


def chain(arrived, label, sources, per, mine, lanes):
    square = (lanes, lanes)
    count = sources * per
    down_at = lax.broadcasted_iota(jnp.int32, square, 0)
    across_at = lax.broadcasted_iota(jnp.int32, square, 1)
    sender, local_slot = down_at // per, down_at % per

    def add(u, held):
        row = jnp.broadcast_to(arrived[u, label : label + 1, :], square)
        return jnp.where(sender == u, row, held)

    held = lax.fori_loop(0, sources, add, jnp.zeros(square, jnp.int32))
    picked = jnp.where(across_at == mine * per + local_slot, held, 0)
    down = jnp.broadcast_to(jnp.sum(picked, axis=1, keepdims=True), square)
    down = jnp.where(down_at < count, down, -1)
    order_down = (mine - sender + sources) % sources * per + local_slot
    order_across = (mine - across_at // per + sources) % sources * per + across_at % per
    earlier = (down.T == down) & (order_down < order_across) & (down_at < count)
    previous = jnp.max(jnp.where(earlier, order_down, -1), axis=0, keepdims=True)
    last = jnp.max(jnp.where(down == across_at, order_down, -1), axis=0, keepdims=True)
    return jnp.where(previous < 0, count, previous), jnp.where(last < 0, count, last)


def coarsen(
    n,
    groups,
    ids_two,
    ids_three,
    blocks,
    labels,
    weight,
    match_one,
    match_two,
    match_three,
    coarse,
    relative,
    land,
    land_labels,
    land_far,
    land_weight,
    near_weight,
    land_weight_far,
    plan,
    plan_smem,
    labels_smem,
    coarse_weight,
    sums_one,
    out_two,
    out_scale_two,
    land_two,
    land_scale_two,
    sums_two,
    out_three,
    out_scale_three,
    land_three,
    land_scale_three,
    sums_three,
    near_send,
    near_recv,
    far_send,
    far_recv,
    local,
):
    me = lax.axis_index("dev")
    group = lax.axis_index("grp")
    per_one, per_two, per_three = land.shape[1], land_two.shape[1], land_three.shape[1]
    count_one, count_two, count_three = n * per_one, n * per_two, groups * per_three

    def peer(step):
        return lax.rem(me + step, n)

    def source(step):
        return lax.rem(me - step + n, n)

    def far_peer(step):
        return lax.rem(group + step, groups)

    def far_source(step):
        return lax.rem(group - step + groups, groups)

    def near(kind, src, dst, there, here):
        return pltpu.make_async_remote_copy(
            src_ref=src,
            dst_ref=dst,
            send_sem=near_send.at[kind, there],
            recv_sem=near_recv.at[kind, here],
            device_id={"dev": there},
            device_id_type=pl.DeviceIdType.MESH,
        )

    def far(kind, src, dst, there, here):
        return pltpu.make_async_remote_copy(
            src_ref=src,
            dst_ref=dst,
            send_sem=far_send.at[kind, there],
            recv_sem=far_recv.at[kind, here],
            device_id={"grp": there},
            device_id_type=pl.DeviceIdType.MESH,
        )

    def send_labels(v, here):
        return near(0, labels, land_labels.at[here], v, here)

    def send_weight(v, here):
        return near(1, weight, land_weight.at[here], v, here)

    def send_blocks(v, here):
        return near(2, blocks.at[v], land.at[here], v, here)

    def send_codes(v, here):
        return near(3, out_two.at[v], land_two.at[here], v, here)

    def send_scales(v, here):
        return near(4, out_scale_two.at[v], land_scale_two.at[here], v, here)

    def send_labels_far(v, here):
        return far(0, labels, land_far.at[here], v, here)

    def send_weight_far(v, here):
        return far(1, near_weight, land_weight_far.at[here], v, here)

    def send_codes_far(v, here):
        return far(2, out_three.at[v], land_three.at[here], v, here)

    def send_scales_far(v, here):
        return far(3, out_scale_three.at[v], land_scale_three.at[here], v, here)

    near_kinds = (send_labels, send_weight, send_blocks, send_codes, send_scales)
    far_kinds = (send_labels_far, send_weight_far, send_codes_far, send_scales_far)

    own_blocks = pltpu.make_async_copy(blocks.at[me], land.at[me], local.at[0])
    own_blocks.start()
    own_labels = pltpu.make_async_copy(labels, land_labels.at[me], local.at[1])
    own_labels.start()
    own_far = pltpu.make_async_copy(labels, land_far.at[group], local.at[2])
    own_far.start()

    barrier = pltpu.get_barrier_semaphore()

    @pl.loop(1, n)
    def _(step):
        pl.semaphore_signal(
            barrier, inc=1, device_id={"dev": peer(step)}, device_id_type=pl.DeviceIdType.MESH
        )

    @pl.loop(1, groups)
    def _(step):
        pl.semaphore_signal(
            barrier, inc=1, device_id={"grp": far_peer(step)}, device_id_type=pl.DeviceIdType.MESH
        )

    pl.semaphore_wait(barrier, n + groups - 2)

    @pl.loop(1, n)
    def _(step):
        send_labels(peer(step), me).start()
        send_weight(peer(step), me).start()

    @pl.loop(1, groups)
    def _(step):
        send_labels_far(far_peer(step), group).start()

    @pl.loop(1, n)
    def _(step):
        send_blocks(peer(step), me).start()

    block_shape = sums_one.shape[1:]
    sums_one[count_one] = jnp.zeros(block_shape, jnp.float32)
    sums_two[count_two] = jnp.zeros(block_shape, jnp.float32)
    sums_three[count_three] = jnp.zeros(block_shape, jnp.float32)

    own_labels.wait()
    own_far.wait()

    @pl.loop(1, n)
    def _(step):
        send_labels(source(step), source(step)).wait_recv()
        send_weight(source(step), source(step)).wait_recv()

    @pl.loop(1, groups)
    def _(step):
        send_labels_far(far_source(step), far_source(step)).wait_recv()

    labels_down = pltpu.make_async_copy(land_labels, labels_smem, local.at[4])
    labels_down.start()
    lanes = plan.shape[1]
    levels = (
        (land_labels, 2, n, per_one, me),
        (land_labels, 3, n, per_two, me),
        (land_far, 4, groups, per_three, group),
    )
    for level, (arrived, label, sources, per, mine) in enumerate(levels):
        previous, last = chain(arrived, label, sources, per, mine, lanes)
        plan[2 * level + 2 : 2 * level + 3] = previous
        plan[2 * level + 3 : 2 * level + 4] = last
    to_smem = pltpu.make_async_copy(plan, plan_smem, local.at[3])
    to_smem.start()

    held = weight[...]
    for step in range(1, n):
        held = held + land_weight[peer(step)]
    near_weight[...] = held
    position = group * n + me
    owned = [weight[e : e + 1, :] for e in range(weight.shape[0])]
    for table in (match_one, match_two, match_three):
        base = position * len(owned)
        folded = [fold(w, table[pl.ds(base + e, 1), :]) for e, w in enumerate(owned)]
        owned = [folded[e] + folded[e + 1] for e in range(0, len(folded), 2)]
    for e, w in enumerate(owned):
        coarse_weight[e : e + 1, :] = w
    labels_down.wait()
    to_smem.wait()

    def level_one(step):
        u = source(step)
        unroll = math.gcd(per_one, 4)

        @pl.loop(0, per_one // unroll)
        def _(i):
            parts = []
            for j in range(unroll):
                k = i * unroll + j
                row = match_one[pl.ds(labels_smem[u, 0, me * per_one + k], 1), :]
                col = match_one[pl.ds(labels_smem[u, 1, me * per_one + k], 1), :]
                parts.append(project_narrow(land[u, k], row, col))
            for j in range(unroll):
                k = i * unroll + j
                before = sums_one[plan_smem[2, u * per_one + k]]
                sums_one[step * per_one + k] = parts[j] + before

    own_blocks.wait()
    level_one(0)

    @pl.loop(1, n)
    def _(step):
        send_blocks(source(step), source(step)).wait_recv()
        level_one(step)

    def parts_out(v, per, plan_row, ids, table, sums, codes, scales):
        unroll = math.gcd(per, 4)

        @pl.loop(0, per // unroll)
        def _(i):
            parts = []
            for j in range(unroll):
                slot = v * per + i * unroll + j
                row = table[pl.ds(ids[0, slot], 1), :]
                col = table[pl.ds(ids[1, slot], 1), :]
                parts.append(project_wide(sums[plan_smem[plan_row, slot]], row, col))
            for j in range(unroll):
                code, scale = encode(parts[j])
                codes[v, i * unroll + j] = code
                scales[v, i * unroll + j] = scale

    def parts_in(step, u, per, plan_row, codes, scales, sums):
        @pl.loop(0, per)
        def _(k):
            before = sums[plan_smem[plan_row, u * per + k]]
            sums[step * per + k] = decode(codes[u, k], scales[u, k]) + before

    @pl.loop(1, n)
    def _(step):
        v = peer(step)
        parts_out(v, per_two, 3, ids_two, match_two, sums_one, out_two, out_scale_two)
        send_codes(v, me).start()
        send_scales(v, me).start()

    parts_out(me, per_two, 3, ids_two, match_two, sums_one, out_two, out_scale_two)
    parts_in(0, me, per_two, 4, out_two, out_scale_two, sums_two)

    @pl.loop(1, groups)
    def _(step):
        send_weight_far(far_peer(step), group).start()

    @pl.loop(1, n)
    def _(step):
        u = source(step)
        send_codes(u, u).wait_recv()
        send_scales(u, u).wait_recv()
        parts_in(step, u, per_two, 4, land_two, land_scale_two, sums_two)

    @pl.loop(1, groups)
    def _(step):
        v = far_peer(step)
        parts_out(v, per_three, 5, ids_three, match_three, sums_two, out_three, out_scale_three)
        send_codes_far(v, group).start()
        send_scales_far(v, group).start()

    parts_out(group, per_three, 5, ids_three, match_three, sums_two, out_three, out_scale_three)
    parts_in(0, group, per_three, 6, out_three, out_scale_three, sums_three)

    held = near_weight[...]
    for step in range(1, groups):
        send_weight_far(far_source(step), far_source(step)).wait_recv()
        held = held + land_weight_far[far_source(step)]
    total = jnp.sum(jnp.sum(held, axis=0, keepdims=True), axis=1, keepdims=True)
    vertices = relative.shape[0] * n * groups * relative.shape[1]
    relative[...] = coarse_weight[...] * vertices / total

    @pl.loop(1, groups)
    def _(step):
        u = far_source(step)
        send_codes_far(u, u).wait_recv()
        send_scales_far(u, u).wait_recv()
        parts_in(step, u, per_three, 6, land_three, land_scale_three, sums_three)

    @pl.loop(0, coarse.shape[0])
    def _(slot):
        coarse[slot] = sums_three[plan_smem[7, slot]]

    @pl.loop(1, n)
    def _(step):
        for kind in near_kinds:
            kind(peer(step), me).wait_send()

    @pl.loop(1, groups)
    def _(step):
        for kind in far_kinds:
            kind(far_peer(step), group).wait_send()


SMEM = pl.BlockSpec(memory_space=pltpu.SMEM)
VMEM = pl.BlockSpec(memory_space=pltpu.VMEM)
HBM = pl.BlockSpec(memory_space=pl.ANY)
ROWS = 8


def per_device(
    blocks,
    ids_one,
    ids_two,
    ids_three,
    match_one,
    match_two,
    match_three,
    target_one,
    target_two,
    target_three,
    vertex_weights,
):
    n, groups = lax.axis_size("dev"), lax.axis_size("grp")
    count, width = blocks.shape[0], blocks.shape[1]
    lanes = -(-count // width) * width
    rows = (ids_one, target_one[None], target_two[None], target_three[None])
    held = [jnp.pad(r, ((0, 0), (0, lanes - r.shape[1]))) for r in rows]
    labels = jnp.pad(jnp.concatenate(held), ((0, ROWS - 5), (0, 0)))
    owned = vertex_weights.shape[0]
    per_one, per_two, per_three = count // n, count // 2 // n, count // 4 // groups
    block = (width, width)
    near_kinds, far_kinds = 5, 4
    return pl.pallas_call(
        functools.partial(coarsen, n, groups),
        in_specs=[SMEM, SMEM, HBM, VMEM, VMEM, VMEM, VMEM, VMEM],
        out_specs=(VMEM, VMEM),
        out_shape=(
            jax.ShapeDtypeStruct((count // 8,) + block, jnp.float32),
            jax.ShapeDtypeStruct((owned // 8, width), jnp.float32),
        ),
        scratch_shapes=[
            pltpu.VMEM((n, per_one) + block, jnp.bfloat16),
            pltpu.VMEM((n, ROWS, lanes), jnp.int32),
            pltpu.VMEM((groups, ROWS, lanes), jnp.int32),
            pltpu.VMEM((n, owned, width), jnp.float32),
            pltpu.VMEM((owned, width), jnp.float32),
            pltpu.VMEM((groups, owned, width), jnp.float32),
            pltpu.VMEM((ROWS, lanes), jnp.int32),
            pltpu.SMEM((ROWS, lanes), jnp.int32),
            pltpu.SMEM((n, ROWS, lanes), jnp.int32),
            pltpu.VMEM((owned // 8, width), jnp.float32),
            pltpu.VMEM((count + 1,) + block, jnp.float32),
            pltpu.VMEM((n, per_two) + block, jnp.int16),
            pltpu.VMEM((n, per_two, 1, width), jnp.float32),
            pltpu.VMEM((n, per_two) + block, jnp.int16),
            pltpu.VMEM((n, per_two, 1, width), jnp.float32),
            pltpu.VMEM((count // 2 + 1,) + block, jnp.float32),
            pltpu.VMEM((groups, per_three) + block, jnp.int16),
            pltpu.VMEM((groups, per_three, 1, width), jnp.float32),
            pltpu.VMEM((groups, per_three) + block, jnp.int16),
            pltpu.VMEM((groups, per_three, 1, width), jnp.float32),
            pltpu.VMEM((count // 4 + 1,) + block, jnp.float32),
            pltpu.SemaphoreType.DMA((near_kinds, n)),
            pltpu.SemaphoreType.DMA((near_kinds, n)),
            pltpu.SemaphoreType.DMA((far_kinds, groups)),
            pltpu.SemaphoreType.DMA((far_kinds, groups)),
            pltpu.SemaphoreType.DMA((5,)),
        ],
        compiler_params=pltpu.CompilerParams(
            collective_id=0, has_side_effects=True, vmem_limit_bytes=60 * 1024 * 1024
        ),
    )(
        ids_two,
        ids_three,
        blocks.reshape((n, per_one) + block),
        labels,
        vertex_weights,
        match_one,
        match_two,
        match_three,
    )


def solution(mesh):
    both = ("grp", "dev")
    return jax.shard_map(
        per_device,
        mesh=mesh,
        in_specs=(
            P(both, None, None),
            P(None, both),
            P(None, both),
            P(None, both),
            P(),
            P(),
            P(),
            P(both),
            P(both),
            P(both),
            P(both, None),
        ),
        out_specs=(P(both, None, None), P(both, None)),
        check_vma=False,
    )
```

profile of v0, /device:TPU:11, one launch (start us, length us, event | category | flops | bytes accessed | tf_op | source)
XLA Modules:
  0.0 107.1 jit_solution(11159819744851514645)
XLA Ops:
  0.6 0.7 pad_add_fusion
  1.4 0.6 pad.14.labels
  2.0 101.7 %shard_map.122 = (f32[16,128,128]{2,1,0:T(8,128)}, f32[1,128]{1,0:T(1,128)}) custom-call(s32[2,64]{1,0:T(2,128)} %ids_two.1, s32[2,32]{1,0:T(2,128)} %ids_three.1, bf16[8,16,128,128]{3,2,1,0:T(8,128)(2,1)} %bitcast.4, s32[8,128]{1,0:T(8,128)} %pad.14.labels, f32[8,128]{1,0:T(8,128)} %weight.1, s32[256,128]{1,0:T(8,128)} %match_one.1, s32[128,128]{1,0:T(8,128)} %match_two.1, ...), custom_call_target="tpu_custom_call" | custom-call | tf_op jit(solution)/shard_map/pallas_call | solution.py:419
  103.7 2.3 %copy.15 = f32[16,128,128]{2,1,0:T(8,128)} copy(f32[16,128,128]{2,1,0:T(8,128)} %get-tuple-element.4) | data formatting | bytes 2097152
  106.0 1.1 %copy.16 = f32[1,128]{1,0:T(1,128)} copy(f32[1,128]{1,0:T(1,128)} %get-tuple-element.5) | data formatting | bytes 1024
where the time goes:
time: 107 us
  Pallas kernels  102 us (95%)
  local copies, waits for them, and re-layouts  4.01 us (4%)
    pallas_call x1, Pallas kernels, per_device(): pl.pallas_call(functools.partial(coarsen, n, groups), in_specs=[SMEM, SME...  102 us
    unnamed x2, local copies, waits for them, and re-layouts  3.41 us

commit v1 on v0

v1 whole, which is shorter than its diff:
```python
import functools
import math

import jax
import jax.numpy as jnp
from jax import lax
from jax.experimental import pallas as pl
from jax.experimental.pallas import tpu as pltpu
from jax.sharding import PartitionSpec as P

LEVELS = 32767.0
TINY = 1e-30
NT = (((1,), (1,)), ((), ()))
ROWS = 8


def hot(row, rows, base):
    names = lax.broadcasted_iota(jnp.int32, (rows, row.shape[1]), 0) + base
    return (names == row).astype(jnp.bfloat16)


def halves(x):
    high = x.astype(jnp.bfloat16)
    low = (x - high.astype(jnp.float32)).astype(jnp.bfloat16)
    return high, low


def project(block, row, col, rows, base):
    left = hot(row, rows, base)
    halfway = jnp.dot(left, block, preferred_element_type=jnp.float32)
    right = hot(col, col.shape[1], 0)
    both = jnp.concatenate([right, right], axis=1)
    split = jnp.concatenate(halves(halfway), axis=1)
    return lax.dot_general(split, both, NT, preferred_element_type=jnp.float32)


def encode(part):
    peak = jnp.maximum(jnp.max(jnp.abs(part), axis=0, keepdims=True), TINY)
    code = jnp.round(part * (LEVELS / peak)).astype(jnp.int32)
    return code.astype(jnp.int16), peak * (1.0 / LEVELS)


def decode(code, scale):
    return code.astype(jnp.int32).astype(jnp.float32) * scale


def lookup(table, index):
    return jnp.take_along_axis(table, index, axis=1, mode="promise_in_bounds")


def fold(weights, row):
    width = row.shape[1]
    place = lax.broadcasted_iota(jnp.int32, (ROWS, width), 0)
    rest = jnp.broadcast_to(weights, (ROWS, width))
    split = jnp.zeros((ROWS, width), jnp.float32)
    for turn in range(3):
        part = rest.astype(jnp.bfloat16).astype(jnp.float32)
        rest = rest - part
        split = jnp.where(place == turn, part, split)
    right = hot(row, width, 0)
    return lax.dot_general(split.astype(jnp.bfloat16), right, NT, preferred_element_type=jnp.float32)


def column(row):
    lanes = row.shape[1]
    return jnp.broadcast_to(row, (lanes, lanes)).T


def latest(match, order):
    return jnp.max(jnp.where(match, order, -1), axis=0, keepdims=True)


def coarsen(
    n,
    groups,
    across,
    ids_smem,
    blocks,
    ids,
    target_one,
    target_two,
    target_three,
    weight,
    match_one,
    match_two,
    match_three,
    coarse,
    relative,
    table,
    own,
    theirs,
    labels,
    land_labels,
    land_far,
    land_weight,
    near_weight,
    land_weight_far,
    plan,
    plan_smem,
    theirs_smem,
    coarse_weight,
    sums,
    out_one,
    out_scale_one,
    land_one,
    land_scale_one,
    out_two,
    out_scale_two,
    land_two,
    land_scale_two,
    out_three,
    out_scale_three,
    land_three,
    land_scale_three,
    sums_three,
    near_send,
    near_recv,
    far_send,
    far_recv,
    raw_send,
    raw_recv,
    one_send,
    one_recv,
    two_send,
    two_recv,
    three_send,
    three_recv,
    own_sem,
    local,
):
    me = lax.axis_index("dev")
    group = lax.axis_index("grp")
    core, chip = me % 2, me // 2
    sibling = me + 1 - 2 * core
    chips = n // 2
    down = chips // across
    my_x, my_y = chip % across, chip // across
    count = own.shape[0]
    width = own.shape[2]
    rows = width // 2
    lanes = labels.shape[1]
    per_one, per_two, slots_two = count // n, count // 2 // n, count // 4
    per_three = slots_two // groups
    chunks = raw_send.shape[0]
    piece = count // chunks
    quarter = match_three.shape[0]
    sizes = ((across, down), (down, across))

    def peer(step):
        return lax.rem(me + step, n)

    def source(step):
        return lax.rem(me - step + n, n)

    def far_peer(step):
        return lax.rem(group + step, groups)

    def far_source(step):
        return lax.rem(group - step + groups, groups)

    def remote(src, dst, send, recv, device):
        return pltpu.make_async_remote_copy(
            src_ref=src,
            dst_ref=dst,
            send_sem=send,
            recv_sem=recv,
            device_id=device,
            device_id_type=pl.DeviceIdType.MESH,
        )

    def send_labels(v, here):
        return remote(labels, land_labels.at[here], near_send.at[0, v], near_recv.at[0, here], {"dev": v})

    def send_weight(v, here):
        return remote(weight, land_weight.at[here], near_send.at[1, v], near_recv.at[1, here], {"dev": v})

    def send_labels_far(v, here):
        return remote(labels, land_far.at[here], far_send.at[0, v], far_recv.at[0, here], {"grp": v})

    def send_weight_far(v, here):
        return remote(
            near_weight, land_weight_far.at[here], far_send.at[1, v], far_recv.at[1, here], {"grp": v}
        )

    def own_copy(c):
        return pltpu.make_async_copy(
            blocks.at[pl.ds(c * piece, piece)], own.at[pl.ds(c * piece, piece)], own_sem.at[c]
        )

    def send_raw(c):
        return remote(
            own.at[pl.ds(c * piece, piece)],
            theirs.at[pl.ds(c * piece, piece)],
            raw_send.at[c],
            raw_recv.at[c],
            {"dev": sibling},
        )

    def chip_at(b, first, second):
        return second * across + first if b == 0 else first * across + second

    def here_of(b):
        return (my_x, my_y) if b == 0 else (my_y, my_x)

    def send_one(i, b, step, turn):
        z, w = sizes[b]
        first, second = here_of(b)
        m = (step - 1) * w + turn
        to = chip_at(b, (first + step) % z, second) * 2 + core
        return (
            remote(
                out_one.at[i, b, m], land_one.at[i, b, m], one_send.at[i, b, m, 0],
                one_recv.at[i, b, m, 0], {"dev": to},
            ),
            remote(
                out_scale_one.at[i, b, m], land_scale_one.at[i, b, m], one_send.at[i, b, m, 1],
                one_recv.at[i, b, m, 1], {"dev": to},
            ),
        )

    def send_two(i, b, turn):
        w = sizes[b][1]
        first, second = here_of(b)
        m = turn - 1
        to = chip_at(b, first, (second + turn) % w) * 2 + core
        return (
            remote(
                out_two.at[i, b, m], land_two.at[i, b, m], two_send.at[i, b, m, 0],
                two_recv.at[i, b, m, 0], {"dev": to},
            ),
            remote(
                out_scale_two.at[i, b, m], land_scale_two.at[i, b, m], two_send.at[i, b, m, 1],
                two_recv.at[i, b, m, 1], {"dev": to},
            ),
        )

    def send_three(i, b, to_group, from_group, from_core):
        device = {"grp": to_group, "dev": chip * 2 + b}
        return (
            remote(
                out_three.at[i, b], land_three.at[from_group, from_core], three_send.at[i, b, 0],
                three_recv.at[from_group, from_core, 0], device,
            ),
            remote(
                out_scale_three.at[i, b], land_scale_three.at[from_group, from_core],
                three_send.at[i, b, 1], three_recv.at[from_group, from_core, 1], device,
            ),
        )

    def chunk_group(i):
        falling = groups - 1 - i
        low = jnp.where(falling > group, falling, falling - 1)
        high = jnp.where(i < group, i, i + 1)
        other = jnp.where(group < groups // 2, low, high)
        return jnp.where(i == groups - 1, group, other)

    for c in range(chunks):
        own_copy(c).start()

    barrier = pltpu.get_barrier_semaphore()

    @pl.loop(1, n)
    def _(step):
        pl.semaphore_signal(
            barrier, inc=1, device_id={"dev": peer(step)}, device_id_type=pl.DeviceIdType.MESH
        )

    @pl.loop(1, groups)
    def _(step):
        v = far_peer(step)
        pl.semaphore_signal(
            barrier, inc=1, device_id={"grp": v}, device_id_type=pl.DeviceIdType.MESH
        )
        pl.semaphore_signal(
            barrier, inc=1, device_id={"grp": v, "dev": sibling}, device_id_type=pl.DeviceIdType.MESH
        )

    labels[...] = jnp.zeros(labels.shape, jnp.int32)
    labels[0:2, 0:count] = ids[...]
    labels[2:3, 0:count] = target_one[...]
    labels[3:4, 0 : count // 2] = target_two[...]
    labels[4:5, 0 : count // 4] = target_three[...]
    land_labels[me] = labels[...]
    land_far[group] = labels[...]

    pl.semaphore_wait(barrier, n - 1 + 2 * (groups - 1))

    @pl.loop(1, n)
    def _(step):
        send_labels(peer(step), me).start()
        send_weight(peer(step), me).start()

    @pl.loop(1, groups)
    def _(step):
        send_labels_far(far_peer(step), group).start()

    for c in range(chunks):
        own_copy(c).wait()
        send_raw(c).start()

    for turn in range(4):
        one = match_one[pl.ds(turn, quarter, stride=4), :]
        two = match_two[pl.ds(turn // 2, quarter, stride=2), :]
        table[turn * quarter : (turn + 1) * quarter, :] = lookup(match_three[...], lookup(two, one))

    def mapping(b):
        return table[pl.ds((b % 4) * quarter + b // 4, 1), :]

    base = core * rows
    sums[2 * count] = jnp.zeros((rows, width), jnp.float32)
    sums_three[groups * per_three] = jnp.zeros(sums_three.shape[1:], jnp.float32)
    unroll = math.gcd(piece, 4)

    @pl.loop(0, count // unroll)
    def _(i):
        for j in range(unroll):
            k = i * unroll + j
            row, col = mapping(ids_smem[0, k]), mapping(ids_smem[1, k])
            sums[k] = project(own[k], row, col, rows, base)

    @pl.loop(1, n)
    def _(step):
        send_labels(source(step), source(step)).wait_recv()
        send_weight(source(step), source(step)).wait_recv()

    @pl.loop(1, groups)
    def _(step):
        send_labels_far(far_source(step), far_source(step)).wait_recv()

    ids_down = pltpu.make_async_copy(land_labels.at[sibling], theirs_smem, local.at[0])
    ids_down.start()

    square = (lanes, lanes)
    lane = lax.broadcasted_iota(jnp.int32, (1, lanes), 1)
    order_down = lax.broadcasted_iota(jnp.int32, square, 0)
    order_across = lax.broadcasted_iota(jnp.int32, square, 1)

    def slots_of(mine):
        first = mine[2:3, :]
        spread = jnp.broadcast_to(first, mine.shape)
        second = jnp.zeros((1, lanes), jnp.int32)
        for o in range(n):
            second = jnp.where(lane // per_one == o, lookup(land_labels[o], spread)[3:4, :], second)
        return first // per_two * slots_two + second

    slot_own, slot_theirs = slots_of(labels[...]), slots_of(land_labels[sibling])
    down_own, down_theirs = column(slot_own), column(slot_theirs)
    none = 2 * count
    before = latest((down_own == slot_own) & (order_down < order_across), order_down)
    plan[0:1, :] = jnp.where(before < 0, none, before)
    before = jnp.maximum(
        latest((down_theirs == slot_theirs) & (order_down < order_across), order_down + count),
        latest(down_own == slot_theirs, order_down),
    )
    plan[1:2, :] = jnp.where(before < 0, none, before)
    blocks_of_slots = -(-n * slots_two // lanes)
    for part in range(blocks_of_slots):
        name = order_across + part * lanes
        last = jnp.maximum(
            latest(down_own == name, order_down), latest(down_theirs == name, order_down + count)
        )
        plan[2 + part : 3 + part, :] = jnp.where(last < 0, none, last)
    total = groups * per_three
    pick = jnp.broadcast_to(group * per_three + lane % per_three, (ROWS, lanes))
    third = jnp.full((1, lanes), -1, jnp.int32)
    for u in range(groups):
        third = jnp.where(lane // per_three == u, lookup(land_far[u], pick)[4:5, :], third)
    down_third = column(third)

    def rank(k):
        return (group - k // per_three - 1 + groups) % groups * per_three + k % per_three

    rank_down, rank_across = rank(order_down), rank(order_across)
    real = order_down < total
    before = latest(real & (down_third == third) & (rank_down < rank_across), rank_down)
    last = latest(real & (down_third == order_across), rank_down)
    third_row = 2 + blocks_of_slots
    plan[third_row : third_row + 1, :] = jnp.where(before < 0, total, before)
    plan[third_row + 1 : third_row + 2, :] = jnp.where(last < 0, total, last)
    rest = plan.shape[0] - third_row - 2
    if rest:
        plan[third_row + 2 :, :] = jnp.zeros((rest, lanes), jnp.int32)
    to_smem = pltpu.make_async_copy(plan, plan_smem, local.at[1])
    to_smem.start()

    held = weight[...]
    for step in range(1, n):
        held = held + land_weight[peer(step)]
    near_weight[...] = held

    @pl.loop(1, groups)
    def _(step):
        send_weight_far(far_peer(step), group).start()

    ids_down.wait()
    to_smem.wait()

    @pl.loop(0, count)
    def _(k):
        sums[k] = sums[k] + sums[plan_smem[0, k]]

    @pl.loop(0, chunks)
    def _(c):
        send_raw(c).wait_recv()

        @pl.loop(0, piece // unroll)
        def _(i):
            parts = []
            for j in range(unroll):
                k = c * piece + i * unroll + j
                row, col = mapping(theirs_smem[0, k]), mapping(theirs_smem[1, k])
                parts.append(project(theirs[k], row, col, rows, base))
            for j in range(unroll):
                k = c * piece + i * unroll + j
                sums[count + k] = parts[j] + sums[plan_smem[1, k]]

    def held_here(to_chip, b, i, j):
        slot = (to_chip * 2 + b) * slots_two + chunk_group(i) * per_three + j
        return sums[plan_smem[2 + slot // lanes, slot % lanes]]

    def pack(parts, codes, scales):
        for j, part in enumerate(parts):
            code, scale = encode(part)
            codes[j] = code
            scales[j : j + 1, :] = scale

    def start(copies):
        for copy in copies:
            copy.start()

    def arrive(copies):
        for copy in copies:
            copy.wait_recv()

    def turns(b):
        w = sizes[b][1]
        return [*range(1, w), 0]

    def first_hop(i):
        for spot in range(max(across, down)):
            for b in range(2):
                z, w = sizes[b]
                if spot >= w:
                    continue
                turn = turns(b)[spot]
                first, second = here_of(b)
                for step in range(1, z):
                    to = chip_at(b, (first + step) % z, (second + turn) % w)
                    m = (step - 1) * w + turn
                    parts = [held_here(to, b, i, j) for j in range(per_three)]
                    pack(parts, out_one.at[i, b, m], out_scale_one.at[i, b, m])
                    start(send_one(i, b, step, turn))

    def with_first(parts, i, b, turn):
        z, w = sizes[b]
        for step in range(1, z):
            m = (step - 1) * w + turn
            arrive(send_one(i, b, step, turn))
            parts = [
                p + decode(land_one[i, b, m, j], land_scale_one[i, b, m, j : j + 1, :])
                for j, p in enumerate(parts)
            ]
        return parts

    def second_hop(i):
        for b in range(2):
            w = sizes[b][1]
            first, second = here_of(b)
            for turn in range(1, w):
                to = chip_at(b, first, (second + turn) % w)
                parts = [held_here(to, b, i, j) for j in range(per_three)]
                parts = with_first(parts, i, b, turn)
                pack(parts, out_two.at[i, b, turn - 1], out_scale_two.at[i, b, turn - 1])
                start(send_two(i, b, turn))

    def reduced(i):
        for b in range(2):
            w = sizes[b][1]
            parts = [held_here(chip, b, i, j) for j in range(per_three)]
            parts = with_first(parts, i, b, 0)
            for turn in range(1, w):
                arrive(send_two(i, b, turn))
                parts = [
                    p + decode(land_two[i, b, turn - 1, j], land_scale_two[i, b, turn - 1, j : j + 1, :])
                    for j, p in enumerate(parts)
                ]
            pack(parts, out_three.at[i, b], out_scale_three.at[i, b])

    def third_hop(i):
        reduced(i)
        for b in range(2):
            start(send_three(i, b, chunk_group(i), group, core))

    @pl.loop(0, groups)
    def _(i):
        first_hop(i)

        @pl.when(i > 0)
        def _():
            third_hop(i - 1)

        second_hop(i)

    owned = weight.shape[0]
    start_row = (group * n + me) * (owned // 4)
    for e in range(owned // 8):
        folded = jnp.zeros((ROWS, width), jnp.float32)
        for f in range(8 * e, 8 * e + 8):
            row = table[pl.ds(f % 4 * quarter + start_row + f // 4, 1), :]
            folded = folded + fold(weight[f : f + 1, :], row)
        coarse_weight[e : e + 1, :] = jnp.sum(folded, axis=0, keepdims=True)
    held = near_weight[...]
    for step in range(1, groups):
        send_weight_far(far_source(step), far_source(step)).wait_recv()
        held = held + land_weight_far[far_source(step)]
    whole = jnp.sum(jnp.sum(held, axis=0, keepdims=True), axis=1, keepdims=True)
    vertices = relative.shape[0] * n * groups * relative.shape[1]
    relative[...] = coarse_weight[...] * vertices / whole

    end = groups - 1
    reduced(end)
    start(send_three(end, 1 - core, group, group, core))

    def take(codes, scales, at, h, u):
        for j in range(per_three):
            part = decode(codes[j], scales[j : j + 1, :])
            sums_three[at + j, h] = part + sums_three[plan_smem[third_row, u * per_three + j], h]

    @pl.loop(1, groups)
    def _(step):
        u = far_source(step)
        for h in range(2):
            arrive(send_three(0, h, u, u, h))
            take(land_three.at[u, h], land_scale_three.at[u, h], (step - 1) * per_three, h, u)

    take(out_three.at[end, core], out_scale_three.at[end, core], end * per_three, core, group)
    other = 1 - core
    arrive(send_three(end, other, group, group, other))
    take(land_three.at[group, other], land_scale_three.at[group, other], end * per_three, other, group)

    @pl.loop(0, coarse.shape[0])
    def _(slot):
        coarse[slot] = sums_three[plan_smem[third_row + 1, slot]]

    @pl.loop(1, n)
    def _(step):
        send_labels(peer(step), me).wait_send()
        send_weight(peer(step), me).wait_send()

    @pl.loop(1, groups)
    def _(step):
        send_labels_far(far_peer(step), group).wait_send()
        send_weight_far(far_peer(step), group).wait_send()

    @pl.loop(0, chunks)
    def _(c):
        send_raw(c).wait_send()

    def sent(copies):
        for copy in copies:
            copy.wait_send()

    @pl.loop(0, groups)
    def _(i):
        for b in range(2):
            z, w = sizes[b]
            for step in range(1, z):
                for turn in range(w):
                    sent(send_one(i, b, step, turn))
            for turn in range(1, w):
                sent(send_two(i, b, turn))

    @pl.loop(0, groups - 1)
    def _(i):
        for b in range(2):
            sent(send_three(i, b, group, group, core))

    sent(send_three(end, 1 - core, group, group, core))


SMEM = pl.BlockSpec(memory_space=pltpu.SMEM)
VMEM = pl.BlockSpec(memory_space=pltpu.VMEM)
HBM = pl.BlockSpec(memory_space=pl.ANY)


def per_device(
    blocks,
    ids_one,
    ids_two,
    ids_three,
    match_one,
    match_two,
    match_three,
    target_one,
    target_two,
    target_three,
    vertex_weights,
):
    n, groups = lax.axis_size("dev"), lax.axis_size("grp")
    count, width = blocks.shape[0], blocks.shape[1]
    rows = width // 2
    lanes = -(-count // width) * width
    owned = vertex_weights.shape[0]
    slots = count // 4
    per = slots // groups
    chips = n // 2
    across = 1
    while across * across < chips:
        across *= 2
    down = chips // across
    hop_one = max((across - 1) * down, (down - 1) * across, 1)
    hop_two = max(across - 1, down - 1, 1)
    plan_rows = -(-(4 + -(-n * slots // lanes)) // ROWS) * ROWS
    chunks = math.gcd(count, 8)
    code = (per, rows, width)

    def message(*lead):
        return [pltpu.VMEM(lead + code, jnp.int16), pltpu.VMEM(lead + (per, width), jnp.float32)] * 2

    coarse, relative = pl.pallas_call(
        functools.partial(coarsen, n, groups, across),
        in_specs=[SMEM, HBM] + [VMEM] * 8,
        out_specs=(VMEM, VMEM),
        out_shape=(
            jax.ShapeDtypeStruct((count // 8, 2, rows, width), jnp.float32),
            jax.ShapeDtypeStruct((owned // 8, width), jnp.float32),
        ),
        scratch_shapes=[
            pltpu.VMEM(match_one.shape, jnp.int32),
            pltpu.VMEM((count, width, width), jnp.bfloat16),
            pltpu.VMEM((count, width, width), jnp.bfloat16),
            pltpu.VMEM((ROWS, lanes), jnp.int32),
            pltpu.VMEM((n, ROWS, lanes), jnp.int32),
            pltpu.VMEM((groups, ROWS, lanes), jnp.int32),
            pltpu.VMEM((n, owned, width), jnp.float32),
            pltpu.VMEM((owned, width), jnp.float32),
            pltpu.VMEM((groups, owned, width), jnp.float32),
            pltpu.VMEM((plan_rows, lanes), jnp.int32),
            pltpu.SMEM((plan_rows, lanes), jnp.int32),
            pltpu.SMEM((ROWS, lanes), jnp.int32),
            pltpu.VMEM((owned // 8, width), jnp.float32),
            pltpu.VMEM((2 * count + 1, rows, width), jnp.float32),
            *message(groups, 2, hop_one),
            *message(groups, 2, hop_two),
            *message(groups, 2),
            pltpu.VMEM((groups * per + 1, 2, rows, width), jnp.float32),
            pltpu.SemaphoreType.DMA((2, n)),
            pltpu.SemaphoreType.DMA((2, n)),
            pltpu.SemaphoreType.DMA((2, groups)),
            pltpu.SemaphoreType.DMA((2, groups)),
            pltpu.SemaphoreType.DMA((chunks,)),
            pltpu.SemaphoreType.DMA((chunks,)),
            pltpu.SemaphoreType.DMA((groups, 2, hop_one, 2)),
            pltpu.SemaphoreType.DMA((groups, 2, hop_one, 2)),
            pltpu.SemaphoreType.DMA((groups, 2, hop_two, 2)),
            pltpu.SemaphoreType.DMA((groups, 2, hop_two, 2)),
            pltpu.SemaphoreType.DMA((groups, 2, 2)),
            pltpu.SemaphoreType.DMA((groups, 2, 2)),
            pltpu.SemaphoreType.DMA((chunks,)),
            pltpu.SemaphoreType.DMA((2,)),
        ],
        compiler_params=pltpu.CompilerParams(
            collective_id=0, has_side_effects=True, vmem_limit_bytes=63 * 1024 * 1024
        ),
    )(
        ids_one,
        blocks,
        ids_one,
        target_one[None],
        target_two[None],
        target_three[None],
        vertex_weights,
        match_one,
        match_two,
        match_three,
    )
    return coarse.reshape(count // 8, width, width), relative


def solution(mesh):
    both = ("grp", "dev")
    return jax.shard_map(
        per_device,
        mesh=mesh,
        in_specs=(
            P(both, None, None),
            P(None, both),
            P(None, both),
            P(None, both),
            P(),
            P(),
            P(),
            P(both),
            P(both),
            P(both),
            P(both, None),
        ),
        out_specs=(P(both, None, None), P(both, None)),
        check_vma=False,
    )
```

time: 107 us -> 78.5 us (0.73)
  the two profiles are of different devices: /device:TPU:11 before, /device:TPU:1 now
where the time goes in v1:
time: 78.5 us; the launch traced here: 78.3 us
  Pallas kernels  74.3 us (95%)
  local copies, waits for them, and re-layouts  3.41 us (4%)
    pallas_call x1, Pallas kernels, per_device(): pl.pallas_call(functools.partial(coarsen, n, groups, across), in_specs=[S...  74.3 us
    unnamed x2, local copies, waits for them, and re-layouts  3.41 us

profile of v1, /device:TPU:1, one launch (start us, length us, event | category | flops | bytes accessed | tf_op | source)
XLA Modules:
  0.0 78.3 jit_solution(6132575741611337641)
XLA Ops:
  0.6 74.3 %shard_map.104 = (f32[16,2,64,128]{3,2,1,0:T(8,128)}, f32[1,128]{1,0:T(1,128)}) custom-call(s32[2,128]{1,0:T(2,128)} %ids.1, bf16[128,128,128]{2,1,0:T(8,128)(2,1)} %blocks.1, s32[2,128]{1,0:T(2,128)} %ids.1, s32[1,128]{1,0:T(1,128)} %bitcast.5, s32[1,64]{1,0:T(1,128)} %bitcast.6, s32[1,32]{1,0:T(1,128)} %bitcast.7, f32[8,128]{1,0:T(8,128)} %weight.1, ...), custom_call_target="tpu_custom_call" | custom-call | tf_op jit(solution)/shard_map/pallas_call | solution.py:620
  74.9 2.3 %copy.13 = f32[16,128,128]{2,1,0:T(8,128)} copy(f32[16,128,128]{2,1,0:T(8,128)} %bitcast.4) | data formatting | bytes 2097152
  77.2 1.1 %copy.14 = f32[1,128]{1,0:T(1,128)} copy(f32[1,128]{1,0:T(1,128)} %get-tuple-element.9) | data formatting | bytes 1024

commit v2 on v1

--- a/solution.py
+++ b/solution.py
@@ -309,14 +309,17 @@
     base = core * rows
     sums[2 * count] = jnp.zeros((rows, width), jnp.float32)
     sums_three[groups * per_three] = jnp.zeros(sums_three.shape[1:], jnp.float32)
-    unroll = math.gcd(piece, 4)
+    unroll = math.gcd(piece, 16)
 
     @pl.loop(0, count // unroll)
     def _(i):
+        parts = []
         for j in range(unroll):
             k = i * unroll + j
             row, col = mapping(ids_smem[0, k]), mapping(ids_smem[1, k])
-            sums[k] = project(own[k], row, col, rows, base)
+            parts.append(project(own[k], row, col, rows, base))
+        for j in range(unroll):
+            sums[i * unroll + j] = parts[j]
 
     @pl.loop(1, n)
     def _(step):
@@ -395,9 +398,11 @@
     ids_down.wait()
     to_smem.wait()
 
-    @pl.loop(0, count)
-    def _(k):
-        sums[k] = sums[k] + sums[plan_smem[0, k]]
+    @pl.loop(0, count // unroll)
+    def _(i):
+        for j in range(unroll):
+            k = i * unroll + j
+            sums[k] = sums[k] + sums[plan_smem[0, k]]
 
     @pl.loop(0, chunks)
     def _(c):

time: 78.5 us -> 70.3 us (0.90)
  Pallas kernels: 74.3 us -> 66 us
    pallas_call x1, Pallas kernels: 74.3 us -> 66 us  [per_device(): pl.pallas_call(functools.partial(coarsen, n, groups, across), in_specs=[S...]
where the time goes in v2:
time: 70.3 us; the launch traced here: 70.1 us
  Pallas kernels  66 us (94%)
  local copies, waits for them, and re-layouts  3.41 us (5%)
    pallas_call x1, Pallas kernels, per_device(): pl.pallas_call(functools.partial(coarsen, n, groups, across), in_specs=[S...  66 us
    unnamed x2, local copies, waits for them, and re-layouts  3.41 us

profile of v2, /device:TPU:1, one launch (start us, length us, event | category | flops | bytes accessed | tf_op | source)
XLA Modules:
  0.0 70.1 jit_solution(8474604616002024278)
XLA Ops:
  0.6 66.0 %shard_map.104 = (f32[16,2,64,128]{3,2,1,0:T(8,128)}, f32[1,128]{1,0:T(1,128)}) custom-call(s32[2,128]{1,0:T(2,128)} %ids.1, bf16[128,128,128]{2,1,0:T(8,128)(2,1)} %blocks.1, s32[2,128]{1,0:T(2,128)} %ids.1, s32[1,128]{1,0:T(1,128)} %bitcast.5, s32[1,64]{1,0:T(1,128)} %bitcast.6, s32[1,32]{1,0:T(1,128)} %bitcast.7, f32[8,128]{1,0:T(8,128)} %weight.1, ...), custom_call_target="tpu_custom_call" | custom-call | tf_op jit(solution)/shard_map/pallas_call | solution.py:625
  66.7 2.3 %copy.13 = f32[16,128,128]{2,1,0:T(8,128)} copy(f32[16,128,128]{2,1,0:T(8,128)} %bitcast.4) | data formatting | bytes 2097152
  69.0 1.1 %copy.14 = f32[1,128]{1,0:T(1,128)} copy(f32[1,128]{1,0:T(1,128)} %get-tuple-element.9) | data formatting | bytes 1024

commit v3 on v2

--- a/solution.py
+++ b/solution.py
@@ -14,8 +14,8 @@
 ROWS = 8
 
 
-def hot(row, rows, base):
-    names = lax.broadcasted_iota(jnp.int32, (rows, row.shape[1]), 0) + base
+def hot(row, rows):
+    names = lax.broadcasted_iota(jnp.int32, (rows, row.shape[1]), 0)
     return (names == row).astype(jnp.bfloat16)
 
 
@@ -25,10 +25,10 @@
     return high, low
 
 
-def project(block, row, col, rows, base):
-    left = hot(row, rows, base)
+def project(block, row, col):
+    left = hot(row, row.shape[1])
     halfway = jnp.dot(left, block, preferred_element_type=jnp.float32)
-    right = hot(col, col.shape[1], 0)
+    right = hot(col, col.shape[1])
     both = jnp.concatenate([right, right], axis=1)
     split = jnp.concatenate(halves(halfway), axis=1)
     return lax.dot_general(split, both, NT, preferred_element_type=jnp.float32)
@@ -57,7 +57,7 @@
         part = rest.astype(jnp.bfloat16).astype(jnp.float32)
         rest = rest - part
         split = jnp.where(place == turn, part, split)
-    right = hot(row, width, 0)
+    right = hot(row, width)
     return lax.dot_general(split.astype(jnp.bfloat16), right, NT, preferred_element_type=jnp.float32)
 
 
@@ -88,7 +88,6 @@
     relative,
     table,
     own,
-    theirs,
     labels,
     land_labels,
     land_far,
@@ -97,9 +96,12 @@
     land_weight_far,
     plan,
     plan_smem,
-    theirs_smem,
     coarse_weight,
     sums,
+    out_half,
+    out_scale_half,
+    land_half,
+    land_scale_half,
     out_one,
     out_scale_one,
     land_one,
@@ -117,8 +119,8 @@
     near_recv,
     far_send,
     far_recv,
-    raw_send,
-    raw_recv,
+    half_send,
+    half_recv,
     one_send,
     one_recv,
     two_send,
@@ -127,6 +129,7 @@
     three_recv,
     own_sem,
     local,
+    free,
 ):
     me = lax.axis_index("dev")
     group = lax.axis_index("grp")
@@ -141,9 +144,11 @@
     lanes = labels.shape[1]
     per_one, per_two, slots_two = count // n, count // 2 // n, count // 4
     per_three = slots_two // groups
-    chunks = raw_send.shape[0]
-    piece = count // chunks
     quarter = match_three.shape[0]
+    ring = out_half.shape[0]
+    trips = own_sem.shape[0]
+    unroll = count // trips
+    middle = trips * 3 // 4
     sizes = ((across, down), (down, across))
 
     def peer(step):
@@ -182,18 +187,21 @@
             near_weight, land_weight_far.at[here], far_send.at[1, v], far_recv.at[1, here], {"grp": v}
         )
 
-    def own_copy(c):
-        return pltpu.make_async_copy(
-            blocks.at[pl.ds(c * piece, piece)], own.at[pl.ds(c * piece, piece)], own_sem.at[c]
-        )
-
-    def send_raw(c):
-        return remote(
-            own.at[pl.ds(c * piece, piece)],
-            theirs.at[pl.ds(c * piece, piece)],
-            raw_send.at[c],
-            raw_recv.at[c],
-            {"dev": sibling},
+    def own_copy(i):
+        part = pl.ds(i * unroll, unroll)
+        return pltpu.make_async_copy(blocks.at[part], own.at[part], own_sem.at[i])
+
+    def send_half(i, dx, dy):
+        at, r = i % ring, dy * across + dx
+        return (
+            remote(
+                out_half.at[at, r], land_half.at[at, r], half_send.at[at, r, 0], half_recv.at[at, r, 0],
+                {"dev": sibling},
+            ),
+            remote(
+                out_scale_half.at[at, r], land_scale_half.at[at, r], half_send.at[at, r, 1],
+                half_recv.at[at, r, 1], {"dev": sibling},
+            ),
         )
 
     def chip_at(b, first, second):
@@ -254,8 +262,8 @@
         other = jnp.where(group < groups // 2, low, high)
         return jnp.where(i == groups - 1, group, other)
 
-    for c in range(chunks):
-        own_copy(c).start()
+    for i in range(trips):
+        own_copy(i).start()
 
     barrier = pltpu.get_barrier_semaphore()
 
@@ -280,8 +288,9 @@
     labels[2:3, 0:count] = target_one[...]
     labels[3:4, 0 : count // 2] = target_two[...]
     labels[4:5, 0 : count // 4] = target_three[...]
-    land_labels[me] = labels[...]
-    land_far[group] = labels[...]
+    named = labels[...]
+    land_labels[me] = named
+    land_far[group] = named
 
     pl.semaphore_wait(barrier, n - 1 + 2 * (groups - 1))
 
@@ -293,10 +302,6 @@
     @pl.loop(1, groups)
     def _(step):
         send_labels_far(far_peer(step), group).start()
-
-    for c in range(chunks):
-        own_copy(c).wait()
-        send_raw(c).start()
 
     for turn in range(4):
         one = match_one[pl.ds(turn, quarter, stride=4), :]
@@ -306,20 +311,24 @@
     def mapping(b):
         return table[pl.ds((b % 4) * quarter + b // 4, 1), :]
 
-    base = core * rows
-    sums[2 * count] = jnp.zeros((rows, width), jnp.float32)
+    none = count
+    sums[none] = jnp.zeros(sums.shape[1:], jnp.float32)
     sums_three[groups * per_three] = jnp.zeros(sums_three.shape[1:], jnp.float32)
-    unroll = math.gcd(piece, 16)
-
-    @pl.loop(0, count // unroll)
-    def _(i):
+
+    def level(i, chained):
+        own_copy(i).wait()
         parts = []
         for j in range(unroll):
             k = i * unroll + j
             row, col = mapping(ids_smem[0, k]), mapping(ids_smem[1, k])
-            parts.append(project(own[k], row, col, rows, base))
+            parts.append(project(own[k], row, col))
         for j in range(unroll):
-            sums[i * unroll + j] = parts[j]
+            k = i * unroll + j
+            sums[k] = parts[j] + sums[plan_smem[0, k] if chained else none]
+
+    @pl.loop(0, max(middle - 1, 0))
+    def _(i):
+        level(i, False)
 
     @pl.loop(1, n)
     def _(step):
@@ -329,9 +338,6 @@
     @pl.loop(1, groups)
     def _(step):
         send_labels_far(far_source(step), far_source(step)).wait_recv()
-
-    ids_down = pltpu.make_async_copy(land_labels.at[sibling], theirs_smem, local.at[0])
-    ids_down.start()
 
     square = (lanes, lanes)
     lane = lax.broadcasted_iota(jnp.int32, (1, lanes), 1)
@@ -346,23 +352,15 @@
             second = jnp.where(lane // per_one == o, lookup(land_labels[o], spread)[3:4, :], second)
         return first // per_two * slots_two + second
 
-    slot_own, slot_theirs = slots_of(labels[...]), slots_of(land_labels[sibling])
-    down_own, down_theirs = column(slot_own), column(slot_theirs)
-    none = 2 * count
+    slot_own = slots_of(named)
+    down_own = column(slot_own)
     before = latest((down_own == slot_own) & (order_down < order_across), order_down)
     plan[0:1, :] = jnp.where(before < 0, none, before)
-    before = jnp.maximum(
-        latest((down_theirs == slot_theirs) & (order_down < order_across), order_down + count),
-        latest(down_own == slot_theirs, order_down),
-    )
-    plan[1:2, :] = jnp.where(before < 0, none, before)
     blocks_of_slots = -(-n * slots_two // lanes)
     for part in range(blocks_of_slots):
         name = order_across + part * lanes
-        last = jnp.maximum(
-            latest(down_own == name, order_down), latest(down_theirs == name, order_down + count)
-        )
-        plan[2 + part : 3 + part, :] = jnp.where(last < 0, none, last)
+        last = latest(down_own == name, order_down)
+        plan[1 + part : 2 + part, :] = jnp.where(last < 0, none, last)
     total = groups * per_three
     pick = jnp.broadcast_to(group * per_three + lane % per_three, (ROWS, lanes))
     third = jnp.full((1, lanes), -1, jnp.int32)
@@ -377,7 +375,7 @@
     real = order_down < total
     before = latest(real & (down_third == third) & (rank_down < rank_across), rank_down)
     last = latest(real & (down_third == order_across), rank_down)
-    third_row = 2 + blocks_of_slots
+    third_row = 1 + blocks_of_slots
     plan[third_row : third_row + 1, :] = jnp.where(before < 0, total, before)
     plan[third_row + 1 : third_row + 2, :] = jnp.where(last < 0, total, last)
     rest = plan.shape[0] - third_row - 2
@@ -395,33 +393,64 @@
     def _(step):
         send_weight_far(far_peer(step), group).start()
 
-    ids_down.wait()
+    @pl.loop(max(middle - 1, 0), middle)
+    def _(i):
+        level(i, False)
+
     to_smem.wait()
 
-    @pl.loop(0, count // unroll)
+    @pl.loop(0, middle)
     def _(i):
         for j in range(unroll):
             k = i * unroll + j
             sums[k] = sums[k] + sums[plan_smem[0, k]]
 
-    @pl.loop(0, chunks)
-    def _(c):
-        send_raw(c).wait_recv()
-
-        @pl.loop(0, piece // unroll)
-        def _(i):
-            parts = []
-            for j in range(unroll):
-                k = c * piece + i * unroll + j
-                row, col = mapping(theirs_smem[0, k]), mapping(theirs_smem[1, k])
-                parts.append(project(theirs[k], row, col, rows, base))
-            for j in range(unroll):
-                k = c * piece + i * unroll + j
-                sums[count + k] = parts[j] + sums[plan_smem[1, k]]
-
-    def held_here(to_chip, b, i, j):
+    @pl.loop(middle, trips)
+    def _(i):
+        level(i, True)
+
+    def from_own(to_chip, b, i, j, h):
         slot = (to_chip * 2 + b) * slots_two + chunk_group(i) * per_three + j
-        return sums[plan_smem[2 + slot // lanes, slot % lanes]]
+        spot = plan_smem[1 + slot // lanes, slot % lanes]
+        return sums[spot, pl.ds(pl.multiple_of(h * rows, rows), rows), :]
+
+    def held_here(b, i, dx, dy):
+        to = (my_y + dy) % down * across + (my_x + dx) % across
+        at, r = i % ring, dy * across + dx
+        parts = []
+        for j in range(per_three):
+            m = b * per_three + j
+            part = decode(land_half[at, r, m], land_scale_half[at, r, m : m + 1, :])
+            parts.append(part + from_own(to, b, i, j, core))
+        return parts
+
+    places = [(dx, dy) for dy in range(down) for dx in range(across)]
+    places.sort(key=lambda p: (p[0] == 0) + (p[1] == 0))
+
+    def spread(i):
+        if ring < groups:
+
+            @pl.when(i >= ring)
+            def _():
+                pl.semaphore_wait(free, 1)
+                for dx, dy in places:
+                    sent(send_half(i, dx, dy))
+
+        for dx, dy in places:
+            to = (my_y + dy) % down * across + (my_x + dx) % across
+            at, r = i % ring, dy * across + dx
+            parts = [from_own(to, b, i, j, 1 - core) for b in range(2) for j in range(per_three)]
+            pack(parts, out_half.at[at, r], out_scale_half.at[at, r])
+            start(send_half(i, dx, dy))
+
+    def release(i):
+        if ring < groups:
+
+            @pl.when(i < groups - ring)
+            def _():
+                pl.semaphore_signal(
+                    free, inc=1, device_id={"dev": sibling}, device_id_type=pl.DeviceIdType.MESH
+                )
 
     def pack(parts, codes, scales):
         for j, part in enumerate(parts):
@@ -437,22 +466,32 @@
         for copy in copies:
             copy.wait_recv()
 
+    def sent(copies):
+        for copy in copies:
+            copy.wait_send()
+
+    def offset(b, first, second):
+        return (first, second) if b == 0 else (second, first)
+
     def turns(b):
         w = sizes[b][1]
         return [*range(1, w), 0]
 
     def first_hop(i):
+        here = set()
         for spot in range(max(across, down)):
             for b in range(2):
                 z, w = sizes[b]
                 if spot >= w:
                     continue
                 turn = turns(b)[spot]
-                first, second = here_of(b)
                 for step in range(1, z):
-                    to = chip_at(b, (first + step) % z, (second + turn) % w)
                     m = (step - 1) * w + turn
-                    parts = [held_here(to, b, i, j) for j in range(per_three)]
+                    place = offset(b, step, turn)
+                    if place not in here:
+                        here.add(place)
+                        arrive(send_half(i, *place))
+                    parts = held_here(b, i, *place)
                     pack(parts, out_one.at[i, b, m], out_scale_one.at[i, b, m])
                     start(send_one(i, b, step, turn))
 
@@ -470,18 +509,17 @@
     def second_hop(i):
         for b in range(2):
             w = sizes[b][1]
-            first, second = here_of(b)
             for turn in range(1, w):
-                to = chip_at(b, first, (second + turn) % w)
-                parts = [held_here(to, b, i, j) for j in range(per_three)]
+                parts = held_here(b, i, *offset(b, 0, turn))
                 parts = with_first(parts, i, b, turn)
                 pack(parts, out_two.at[i, b, turn - 1], out_scale_two.at[i, b, turn - 1])
                 start(send_two(i, b, turn))
 
     def reduced(i):
+        arrive(send_half(i, 0, 0))
         for b in range(2):
             w = sizes[b][1]
-            parts = [held_here(chip, b, i, j) for j in range(per_three)]
+            parts = held_here(b, i, 0, 0)
             parts = with_first(parts, i, b, 0)
             for turn in range(1, w):
                 arrive(send_two(i, b, turn))
@@ -490,12 +528,15 @@
                     for j, p in enumerate(parts)
                 ]
             pack(parts, out_three.at[i, b], out_scale_three.at[i, b])
+        release(i)
 
     def third_hop(i):
         reduced(i)
         for b in range(2):
             start(send_three(i, b, chunk_group(i), group, core))
 
+    spread(0)
+
     @pl.loop(0, groups)
     def _(i):
         first_hop(i)
@@ -503,6 +544,10 @@
         @pl.when(i > 0)
         def _():
             third_hop(i - 1)
+
+        @pl.when(i + 1 < groups)
+        def _():
+            spread(i + 1)
 
         second_hop(i)
 
@@ -557,13 +602,10 @@
         send_labels_far(far_peer(step), group).wait_send()
         send_weight_far(far_peer(step), group).wait_send()
 
-    @pl.loop(0, chunks)
-    def _(c):
-        send_raw(c).wait_send()
-
-    def sent(copies):
-        for copy in copies:
-            copy.wait_send()
+    @pl.loop(groups - ring, groups)
+    def _(i):
+        for dx, dy in places:
+            sent(send_half(i, dx, dy))
 
     @pl.loop(0, groups)
     def _(i):
@@ -586,6 +628,7 @@
 SMEM = pl.BlockSpec(memory_space=pltpu.SMEM)
 VMEM = pl.BlockSpec(memory_space=pltpu.VMEM)
 HBM = pl.BlockSpec(memory_space=pl.ANY)
+VMEM_BYTES = 67_043_328
 
 
 def per_device(
@@ -615,12 +658,15 @@
     down = chips // across
     hop_one = max((across - 1) * down, (down - 1) * across, 1)
     hop_two = max(across - 1, down - 1, 1)
-    plan_rows = -(-(4 + -(-n * slots // lanes)) // ROWS) * ROWS
-    chunks = math.gcd(count, 8)
-    code = (per, rows, width)
-
-    def message(*lead):
-        return [pltpu.VMEM(lead + code, jnp.int16), pltpu.VMEM(lead + (per, width), jnp.float32)] * 2
+    plan_rows = -(-(3 + -(-n * slots // lanes)) // ROWS) * ROWS
+    half_bytes = groups * chips * 4 * per * rows * width * 2
+    ring = groups if half_bytes <= VMEM_BYTES // 4 else 2
+
+    def message(*lead, per=per):
+        return [
+            pltpu.VMEM(lead + (per, rows, width), jnp.int16),
+            pltpu.VMEM(lead + (per, width), jnp.float32),
+        ] * 2
 
     coarse, relative = pl.pallas_call(
         functools.partial(coarsen, n, groups, across),
@@ -633,7 +679,6 @@
         scratch_shapes=[
             pltpu.VMEM(match_one.shape, jnp.int32),
             pltpu.VMEM((count, width, width), jnp.bfloat16),
-            pltpu.VMEM((count, width, width), jnp.bfloat16),
             pltpu.VMEM((ROWS, lanes), jnp.int32),
             pltpu.VMEM((n, ROWS, lanes), jnp.int32),
             pltpu.VMEM((groups, ROWS, lanes), jnp.int32),
@@ -642,9 +687,9 @@
             pltpu.VMEM((groups, owned, width), jnp.float32),
             pltpu.VMEM((plan_rows, lanes), jnp.int32),
             pltpu.SMEM((plan_rows, lanes), jnp.int32),
-            pltpu.SMEM((ROWS, lanes), jnp.int32),
             pltpu.VMEM((owned // 8, width), jnp.float32),
-            pltpu.VMEM((2 * count + 1, rows, width), jnp.float32),
+            pltpu.VMEM((count + 1, width, width), jnp.float32),
+            *message(ring, chips, per=2 * per),
             *message(groups, 2, hop_one),
             *message(groups, 2, hop_two),
             *message(groups, 2),
@@ -653,19 +698,22 @@
             pltpu.SemaphoreType.DMA((2, n)),
             pltpu.SemaphoreType.DMA((2, groups)),
             pltpu.SemaphoreType.DMA((2, groups)),
-            pltpu.SemaphoreType.DMA((chunks,)),
-            pltpu.SemaphoreType.DMA((chunks,)),
+            pltpu.SemaphoreType.DMA((ring, chips, 2)),
+            pltpu.SemaphoreType.DMA((ring, chips, 2)),
             pltpu.SemaphoreType.DMA((groups, 2, hop_one, 2)),
             pltpu.SemaphoreType.DMA((groups, 2, hop_one, 2)),
             pltpu.SemaphoreType.DMA((groups, 2, hop_two, 2)),
             pltpu.SemaphoreType.DMA((groups, 2, hop_two, 2)),
             pltpu.SemaphoreType.DMA((groups, 2, 2)),
             pltpu.SemaphoreType.DMA((groups, 2, 2)),
-            pltpu.SemaphoreType.DMA((chunks,)),
+            pltpu.SemaphoreType.DMA((count // math.gcd(count, 16),)),
             pltpu.SemaphoreType.DMA((2,)),
+            pltpu.SemaphoreType.REGULAR,
         ],
         compiler_params=pltpu.CompilerParams(
-            collective_id=0, has_side_effects=True, vmem_limit_bytes=63 * 1024 * 1024
+            collective_id=0,
+            has_side_effects=True,
+            vmem_limit_bytes=VMEM_BYTES,
         ),
     )(
         ids_one,

time: 70.3 us -> 60.8 us (0.86)
  Pallas kernels: 66 us -> 56.6 us
    pallas_call x1, Pallas kernels: 66 us -> 56.6 us  [per_device(): pl.pallas_call(functools.partial(coarsen, n, groups, across), in_specs=[S...]
where the time goes in v3:
time: 60.8 us; the launch traced here: 60.7 us
  Pallas kernels  56.6 us (93%)
  local copies, waits for them, and re-layouts  3.41 us (6%)
  between operations  0.64 us (1%)
    pallas_call x1, Pallas kernels, per_device(): pl.pallas_call(functools.partial(coarsen, n, groups, across), in_specs=[S...  56.6 us
    unnamed x2, local copies, waits for them, and re-layouts  3.41 us

profile of v3, /device:TPU:1, one launch (start us, length us, event | category | flops | bytes accessed | tf_op | source)
XLA Modules:
  0.0 60.7 jit_solution(10823004467217694220)
XLA Ops:
  0.6 56.6 %shard_map.104 = (f32[16,2,64,128]{3,2,1,0:T(8,128)}, f32[1,128]{1,0:T(1,128)}) custom-call(s32[2,128]{1,0:T(2,128)} %ids.1, bf16[128,128,128]{2,1,0:T(8,128)(2,1)} %blocks.1, s32[2,128]{1,0:T(2,128)} %ids.1, s32[1,128]{1,0:T(1,128)} %bitcast.5, s32[1,64]{1,0:T(1,128)} %bitcast.6, s32[1,32]{1,0:T(1,128)} %bitcast.7, f32[8,128]{1,0:T(8,128)} %weight.1, ...), custom_call_target="tpu_custom_call" | custom-call | tf_op jit(solution)/shard_map/pallas_call | solution.py:671
  57.2 2.3 %copy.13 = f32[16,128,128]{2,1,0:T(8,128)} copy(f32[16,128,128]{2,1,0:T(8,128)} %bitcast.4) | data formatting | bytes 2097152
  59.5 1.1 %copy.14 = f32[1,128]{1,0:T(1,128)} copy(f32[1,128]{1,0:T(1,128)} %get-tuple-element.9) | data formatting | bytes 1024

commit v4 on v3

--- a/solution.py
+++ b/solution.py
@@ -96,6 +96,8 @@
     land_weight_far,
     plan,
     plan_smem,
+    plan_third,
+    third_smem,
     coarse_weight,
     sums,
     out_half,
@@ -115,6 +117,8 @@
     land_three,
     land_scale_three,
     sums_three,
+    bulk,
+    bulk_half,
     near_send,
     near_recv,
     far_send,
@@ -173,18 +177,21 @@
             device_id_type=pl.DeviceIdType.MESH,
         )
 
+    def settle(ref, sem):
+        pltpu.make_async_copy(ref, ref, sem).wait()
+
     def send_labels(v, here):
-        return remote(labels, land_labels.at[here], near_send.at[0, v], near_recv.at[0, here], {"dev": v})
+        return remote(labels, land_labels.at[here], near_send.at[0], near_recv.at[0], {"dev": v})
 
     def send_weight(v, here):
-        return remote(weight, land_weight.at[here], near_send.at[1, v], near_recv.at[1, here], {"dev": v})
+        return remote(weight, land_weight.at[here], near_send.at[1], near_recv.at[1], {"dev": v})
 
     def send_labels_far(v, here):
-        return remote(labels, land_far.at[here], far_send.at[0, v], far_recv.at[0, here], {"grp": v})
+        return remote(labels, land_far.at[here], far_send.at[0], far_recv.at[0], {"grp": v})
 
     def send_weight_far(v, here):
         return remote(
-            near_weight, land_weight_far.at[here], far_send.at[1, v], far_recv.at[1, here], {"grp": v}
+            near_weight, land_weight_far.at[here], far_send.at[1], far_recv.at[1], {"grp": v}
         )
 
     def own_copy(i):
@@ -195,12 +202,12 @@
         at, r = i % ring, dy * across + dx
         return (
             remote(
-                out_half.at[at, r], land_half.at[at, r], half_send.at[at, r, 0], half_recv.at[at, r, 0],
+                out_half.at[at, r], land_half.at[at, r], half_send.at[at, 0], half_recv.at[at, r],
                 {"dev": sibling},
             ),
             remote(
-                out_scale_half.at[at, r], land_scale_half.at[at, r], half_send.at[at, r, 1],
-                half_recv.at[at, r, 1], {"dev": sibling},
+                out_scale_half.at[at, r], land_scale_half.at[at, r], half_send.at[at, 1],
+                half_recv.at[at, r], {"dev": sibling},
             ),
         )
 
@@ -217,12 +224,12 @@
         to = chip_at(b, (first + step) % z, second) * 2 + core
         return (
             remote(
-                out_one.at[i, b, m], land_one.at[i, b, m], one_send.at[i, b, m, 0],
-                one_recv.at[i, b, m, 0], {"dev": to},
+                out_one.at[i, b, m], land_one.at[i, b, m], one_send.at[b, 0],
+                one_recv.at[i, b, m], {"dev": to},
             ),
             remote(
-                out_scale_one.at[i, b, m], land_scale_one.at[i, b, m], one_send.at[i, b, m, 1],
-                one_recv.at[i, b, m, 1], {"dev": to},
+                out_scale_one.at[i, b, m], land_scale_one.at[i, b, m], one_send.at[b, 1],
+                one_recv.at[i, b, m], {"dev": to},
             ),
         )
 
@@ -233,12 +240,12 @@
         to = chip_at(b, first, (second + turn) % w) * 2 + core
         return (
             remote(
-                out_two.at[i, b, m], land_two.at[i, b, m], two_send.at[i, b, m, 0],
-                two_recv.at[i, b, m, 0], {"dev": to},
+                out_two.at[i, b, m], land_two.at[i, b, m], two_send.at[b, 0],
+                two_recv.at[i, b, m], {"dev": to},
             ),
             remote(
-                out_scale_two.at[i, b, m], land_scale_two.at[i, b, m], two_send.at[i, b, m, 1],
-                two_recv.at[i, b, m, 1], {"dev": to},
+                out_scale_two.at[i, b, m], land_scale_two.at[i, b, m], two_send.at[b, 1],
+                two_recv.at[i, b, m], {"dev": to},
             ),
         )
 
@@ -246,12 +253,12 @@
         device = {"grp": to_group, "dev": chip * 2 + b}
         return (
             remote(
-                out_three.at[i, b], land_three.at[from_group, from_core], three_send.at[i, b, 0],
-                three_recv.at[from_group, from_core, 0], device,
+                out_three.at[i * 2 + b], land_three.at[from_group, from_core], three_send.at[0],
+                three_recv.at[from_group, from_core], device,
             ),
             remote(
-                out_scale_three.at[i, b], land_scale_three.at[from_group, from_core],
-                three_send.at[i, b, 1], three_recv.at[from_group, from_core, 1], device,
+                out_scale_three.at[i * 2 + b], land_scale_three.at[from_group, from_core],
+                three_send.at[1], three_recv.at[from_group, from_core], device,
             ),
         )
 
@@ -330,14 +337,7 @@
     def _(i):
         level(i, False)
 
-    @pl.loop(1, n)
-    def _(step):
-        send_labels(source(step), source(step)).wait_recv()
-        send_weight(source(step), source(step)).wait_recv()
-
-    @pl.loop(1, groups)
-    def _(step):
-        send_labels_far(far_source(step), far_source(step)).wait_recv()
+    settle(land_labels.at[pl.ds(0, n - 1)], near_recv.at[0])
 
     square = (lanes, lanes)
     lane = lax.broadcasted_iota(jnp.int32, (1, lanes), 1)
@@ -361,37 +361,11 @@
         name = order_across + part * lanes
         last = latest(down_own == name, order_down)
         plan[1 + part : 2 + part, :] = jnp.where(last < 0, none, last)
-    total = groups * per_three
-    pick = jnp.broadcast_to(group * per_three + lane % per_three, (ROWS, lanes))
-    third = jnp.full((1, lanes), -1, jnp.int32)
-    for u in range(groups):
-        third = jnp.where(lane // per_three == u, lookup(land_far[u], pick)[4:5, :], third)
-    down_third = column(third)
-
-    def rank(k):
-        return (group - k // per_three - 1 + groups) % groups * per_three + k % per_three
-
-    rank_down, rank_across = rank(order_down), rank(order_across)
-    real = order_down < total
-    before = latest(real & (down_third == third) & (rank_down < rank_across), rank_down)
-    last = latest(real & (down_third == order_across), rank_down)
-    third_row = 1 + blocks_of_slots
-    plan[third_row : third_row + 1, :] = jnp.where(before < 0, total, before)
-    plan[third_row + 1 : third_row + 2, :] = jnp.where(last < 0, total, last)
-    rest = plan.shape[0] - third_row - 2
+    rest = plan.shape[0] - 1 - blocks_of_slots
     if rest:
-        plan[third_row + 2 :, :] = jnp.zeros((rest, lanes), jnp.int32)
+        plan[1 + blocks_of_slots :, :] = jnp.zeros((rest, lanes), jnp.int32)
     to_smem = pltpu.make_async_copy(plan, plan_smem, local.at[1])
     to_smem.start()
-
-    held = weight[...]
-    for step in range(1, n):
-        held = held + land_weight[peer(step)]
-    near_weight[...] = held
-
-    @pl.loop(1, groups)
-    def _(step):
-        send_weight_far(far_peer(step), group).start()
 
     @pl.loop(max(middle - 1, 0), middle)
     def _(i):
@@ -433,8 +407,8 @@
             @pl.when(i >= ring)
             def _():
                 pl.semaphore_wait(free, 1)
-                for dx, dy in places:
-                    sent(send_half(i, dx, dy))
+                settle(out_half.at[i % ring], half_send.at[i % ring, 0])
+                settle(out_scale_half.at[i % ring], half_send.at[i % ring, 1])
 
         for dx, dy in places:
             to = (my_y + dy) % down * across + (my_x + dx) % across
@@ -461,14 +435,6 @@
     def start(copies):
         for copy in copies:
             copy.start()
-
-    def arrive(copies):
-        for copy in copies:
-            copy.wait_recv()
-
-    def sent(copies):
-        for copy in copies:
-            copy.wait_send()
 
     def offset(b, first, second):
         return (first, second) if b == 0 else (second, first)
@@ -490,7 +456,7 @@
                     place = offset(b, step, turn)
                     if place not in here:
                         here.add(place)
-                        arrive(send_half(i, *place))
+                        settle(bulk_half, half_recv.at[i % ring, place[1] * across + place[0]])
                     parts = held_here(b, i, *place)
                     pack(parts, out_one.at[i, b, m], out_scale_one.at[i, b, m])
                     start(send_one(i, b, step, turn))
@@ -499,7 +465,7 @@
         z, w = sizes[b]
         for step in range(1, z):
             m = (step - 1) * w + turn
-            arrive(send_one(i, b, step, turn))
+            settle(bulk, one_recv.at[i, b, m])
             parts = [
                 p + decode(land_one[i, b, m, j], land_scale_one[i, b, m, j : j + 1, :])
                 for j, p in enumerate(parts)
@@ -516,18 +482,18 @@
                 start(send_two(i, b, turn))
 
     def reduced(i):
-        arrive(send_half(i, 0, 0))
+        settle(bulk_half, half_recv.at[i % ring, 0])
         for b in range(2):
             w = sizes[b][1]
             parts = held_here(b, i, 0, 0)
             parts = with_first(parts, i, b, 0)
             for turn in range(1, w):
-                arrive(send_two(i, b, turn))
+                settle(bulk, two_recv.at[i, b, turn - 1])
                 parts = [
                     p + decode(land_two[i, b, turn - 1, j], land_scale_two[i, b, turn - 1, j : j + 1, :])
                     for j, p in enumerate(parts)
                 ]
-            pack(parts, out_three.at[i, b], out_scale_three.at[i, b])
+            pack(parts, out_three.at[i * 2 + b], out_scale_three.at[i * 2 + b])
         release(i)
 
     def third_hop(i):
@@ -536,6 +502,39 @@
             start(send_three(i, b, chunk_group(i), group, core))
 
     spread(0)
+
+    settle(land_far.at[pl.ds(0, groups - 1)], far_recv.at[0])
+
+    total = groups * per_three
+    pick = jnp.broadcast_to(group * per_three + lane % per_three, (ROWS, lanes))
+    third = jnp.full((1, lanes), -1, jnp.int32)
+    for u in range(groups):
+        third = jnp.where(lane // per_three == u, lookup(land_far[u], pick)[4:5, :], third)
+    down_third = column(third)
+
+    def rank(k):
+        return (group - k // per_three - 1 + groups) % groups * per_three + k % per_three
+
+    rank_down, rank_across = rank(order_down), rank(order_across)
+    real = order_down < total
+    before = latest(real & (down_third == third) & (rank_down < rank_across), rank_down)
+    last = latest(real & (down_third == order_across), rank_down)
+    plan_third[0:1, :] = jnp.where(before < 0, total, before)
+    plan_third[1:2, :] = jnp.where(last < 0, total, last)
+    plan_third[2:, :] = jnp.zeros((plan_third.shape[0] - 2, lanes), jnp.int32)
+    third_to_smem = pltpu.make_async_copy(plan_third, third_smem, local.at[0])
+    third_to_smem.start()
+
+    settle(land_weight.at[pl.ds(0, n - 1)], near_recv.at[1])
+
+    held = weight[...]
+    for step in range(1, n):
+        held = held + land_weight[peer(step)]
+    near_weight[...] = held
+
+    @pl.loop(1, groups)
+    def _(step):
+        send_weight_far(far_peer(step), group).start()
 
     @pl.loop(0, groups)
     def _(i):
@@ -560,13 +559,14 @@
             folded = folded + fold(weight[f : f + 1, :], row)
         coarse_weight[e : e + 1, :] = jnp.sum(folded, axis=0, keepdims=True)
     held = near_weight[...]
+    settle(land_weight_far.at[pl.ds(0, groups - 1)], far_recv.at[1])
     for step in range(1, groups):
-        send_weight_far(far_source(step), far_source(step)).wait_recv()
         held = held + land_weight_far[far_source(step)]
     whole = jnp.sum(jnp.sum(held, axis=0, keepdims=True), axis=1, keepdims=True)
     vertices = relative.shape[0] * n * groups * relative.shape[1]
     relative[...] = coarse_weight[...] * vertices / whole
 
+    third_to_smem.wait()
     end = groups - 1
     reduced(end)
     start(send_three(end, 1 - core, group, group, core))
@@ -574,55 +574,56 @@
     def take(codes, scales, at, h, u):
         for j in range(per_three):
             part = decode(codes[j], scales[j : j + 1, :])
-            sums_three[at + j, h] = part + sums_three[plan_smem[third_row, u * per_three + j], h]
+            sums_three[at + j, h] = part + sums_three[third_smem[0, u * per_three + j], h]
 
     @pl.loop(1, groups)
     def _(step):
         u = far_source(step)
         for h in range(2):
-            arrive(send_three(0, h, u, u, h))
+            settle(bulk, three_recv.at[u, h])
             take(land_three.at[u, h], land_scale_three.at[u, h], (step - 1) * per_three, h, u)
 
-    take(out_three.at[end, core], out_scale_three.at[end, core], end * per_three, core, group)
+    take(out_three.at[end * 2 + core], out_scale_three.at[end * 2 + core], end * per_three, core, group)
     other = 1 - core
-    arrive(send_three(end, other, group, group, other))
+    settle(bulk, three_recv.at[group, other])
     take(land_three.at[group, other], land_scale_three.at[group, other], end * per_three, other, group)
 
     @pl.loop(0, coarse.shape[0])
     def _(slot):
-        coarse[slot] = sums_three[plan_smem[third_row + 1, slot]]
-
-    @pl.loop(1, n)
-    def _(step):
-        send_labels(peer(step), me).wait_send()
-        send_weight(peer(step), me).wait_send()
-
-    @pl.loop(1, groups)
-    def _(step):
-        send_labels_far(far_peer(step), group).wait_send()
-        send_weight_far(far_peer(step), group).wait_send()
-
-    @pl.loop(groups - ring, groups)
-    def _(i):
-        for dx, dy in places:
-            sent(send_half(i, dx, dy))
-
-    @pl.loop(0, groups)
-    def _(i):
-        for b in range(2):
-            z, w = sizes[b]
-            for step in range(1, z):
-                for turn in range(w):
-                    sent(send_one(i, b, step, turn))
-            for turn in range(1, w):
-                sent(send_two(i, b, turn))
-
-    @pl.loop(0, groups - 1)
-    def _(i):
-        for b in range(2):
-            sent(send_three(i, b, group, group, core))
-
-    sent(send_three(end, 1 - core, group, group, core))
+        coarse[slot] = sums_three[third_smem[1, slot]]
+
+    settle(land_labels.at[pl.ds(0, n - 1)], near_send.at[0])
+    settle(land_weight.at[pl.ds(0, n - 1)], near_send.at[1])
+    settle(land_far.at[pl.ds(0, groups - 1)], far_send.at[0])
+    settle(land_weight_far.at[pl.ds(0, groups - 1)], far_send.at[1])
+    for at in range(ring):
+        settle(out_half.at[at], half_send.at[at, 0])
+        settle(out_scale_half.at[at], half_send.at[at, 1])
+    for b in range(2):
+        z, w = sizes[b]
+        some, few = pl.ds(0, (z - 1) * w), pl.ds(0, w - 1)
+        settle(out_one.at[pl.ds(0, groups), b, some], one_send.at[b, 0])
+        settle(out_scale_one.at[pl.ds(0, groups), b, some], one_send.at[b, 1])
+        settle(out_two.at[pl.ds(0, groups), b, few], two_send.at[b, 0])
+        settle(out_scale_two.at[pl.ds(0, groups), b, few], two_send.at[b, 1])
+    settle(out_three.at[pl.ds(0, 2 * groups - 1)], three_send.at[0])
+    settle(out_scale_three.at[pl.ds(0, 2 * groups - 1)], three_send.at[1])
+
+
+def hand_on(coarse_in, relative_in, coarse, relative, blocks, row, arrive, leave):
+    pieces = arrive.shape[0] - 1
+    size = blocks.shape[0] // pieces
+    moves = [(coarse_in, blocks, coarse, pl.ds(i * size, size)) for i in range(pieces)]
+    moves.append((relative_in, row, relative, pl.ds(0, row.shape[0])))
+    ins = [pltpu.make_async_copy(a.at[p], v.at[p], arrive.at[i]) for i, (a, v, _, p) in enumerate(moves)]
+    outs = [pltpu.make_async_copy(v.at[p], b.at[p], leave.at[i]) for i, (_, v, b, p) in enumerate(moves)]
+    for copy in ins:
+        copy.start()
+    for first, second in zip(ins, outs):
+        first.wait()
+        second.start()
+    for copy in outs:
+        copy.wait()
 
 
 SMEM = pl.BlockSpec(memory_space=pltpu.SMEM)
@@ -658,7 +659,7 @@
     down = chips // across
     hop_one = max((across - 1) * down, (down - 1) * across, 1)
     hop_two = max(across - 1, down - 1, 1)
-    plan_rows = -(-(3 + -(-n * slots // lanes)) // ROWS) * ROWS
+    plan_rows = -(-(1 + -(-n * slots // lanes)) // ROWS) * ROWS
     half_bytes = groups * chips * 4 * per * rows * width * 2
     ring = groups if half_bytes <= VMEM_BYTES // 4 else 2
 
@@ -687,25 +688,30 @@
             pltpu.VMEM((groups, owned, width), jnp.float32),
             pltpu.VMEM((plan_rows, lanes), jnp.int32),
             pltpu.SMEM((plan_rows, lanes), jnp.int32),
+            pltpu.VMEM((ROWS, lanes), jnp.int32),
+            pltpu.SMEM((ROWS, lanes), jnp.int32),
             pltpu.VMEM((owned // 8, width), jnp.float32),
             pltpu.VMEM((count + 1, width, width), jnp.float32),
             *message(ring, chips, per=2 * per),
             *message(groups, 2, hop_one),
             *message(groups, 2, hop_two),
-            *message(groups, 2),
+            *message(2 * groups)[:2],
+            *message(groups, 2)[:2],
             pltpu.VMEM((groups * per + 1, 2, rows, width), jnp.float32),
-            pltpu.SemaphoreType.DMA((2, n)),
-            pltpu.SemaphoreType.DMA((2, n)),
-            pltpu.SemaphoreType.DMA((2, groups)),
-            pltpu.SemaphoreType.DMA((2, groups)),
-            pltpu.SemaphoreType.DMA((ring, chips, 2)),
-            pltpu.SemaphoreType.DMA((ring, chips, 2)),
-            pltpu.SemaphoreType.DMA((groups, 2, hop_one, 2)),
-            pltpu.SemaphoreType.DMA((groups, 2, hop_one, 2)),
-            pltpu.SemaphoreType.DMA((groups, 2, hop_two, 2)),
-            pltpu.SemaphoreType.DMA((groups, 2, hop_two, 2)),
-            pltpu.SemaphoreType.DMA((groups, 2, 2)),
-            pltpu.SemaphoreType.DMA((groups, 2, 2)),
+            pltpu.VMEM((per * (rows + 2), width), jnp.int16),
+            pltpu.VMEM((2 * per * (rows + 2), width), jnp.int16),
+            pltpu.SemaphoreType.DMA((2,)),
+            pltpu.SemaphoreType.DMA((2,)),
+            pltpu.SemaphoreType.DMA((2,)),
+            pltpu.SemaphoreType.DMA((2,)),
+            pltpu.SemaphoreType.DMA((ring, 2)),
+            pltpu.SemaphoreType.DMA((ring, chips)),
+            pltpu.SemaphoreType.DMA((2, 2)),
+            pltpu.SemaphoreType.DMA((groups, 2, hop_one)),
+            pltpu.SemaphoreType.DMA((2, 2)),
+            pltpu.SemaphoreType.DMA((groups, 2, hop_two)),
+            pltpu.SemaphoreType.DMA((2,)),
+            pltpu.SemaphoreType.DMA((groups, 2)),
             pltpu.SemaphoreType.DMA((count // math.gcd(count, 16),)),
             pltpu.SemaphoreType.DMA((2,)),
             pltpu.SemaphoreType.REGULAR,
@@ -727,6 +733,22 @@
         match_two,
         match_three,
     )
+    pieces = math.gcd(count // 8, 4)
+    coarse, relative = pl.pallas_call(
+        hand_on,
+        in_specs=[HBM, HBM],
+        out_specs=(HBM, HBM),
+        out_shape=(
+            jax.ShapeDtypeStruct(coarse.shape, jnp.float32),
+            jax.ShapeDtypeStruct(relative.shape, jnp.float32),
+        ),
+        scratch_shapes=[
+            pltpu.VMEM(coarse.shape, jnp.float32),
+            pltpu.VMEM(relative.shape, jnp.float32),
+            pltpu.SemaphoreType.DMA((pieces + 1,)),
+            pltpu.SemaphoreType.DMA((pieces + 1,)),
+        ],
+    )(coarse, relative)
     return coarse.reshape(count // 8, width, width), relative
 
 

time: 60.8 us -> 57.5 us (0.946)
  local copies, waits for them, and re-layouts: 3.41 us -> 0 us
    unnamed x2 -> x0, local copies, waits for them, and re-layouts: 3.41 us -> none
    pallas_call x0 -> x1, Pallas kernels: none -> 2 us  [per_device(): pl.pallas_call(hand_on, in_specs=[HBM, HBM], out_specs=(HBM, HBM), out_sh...]
    pallas_call x1, Pallas kernels: 56.6 us -> 54.7 us  [per_device(): pl.pallas_call(functools.partial(coarsen, n, groups, across), in_specs=[S...]
where the time goes in v4:
time: 57.5 us; the launch traced here: 57.3 us
  Pallas kernels  56.7 us (99%)
  between operations  0.64 us (1%)
    pallas_call x1, Pallas kernels, per_device(): pl.pallas_call(functools.partial(coarsen, n, groups, across), in_specs=[S...  54.7 us
    pallas_call x1, Pallas kernels, per_device(): pl.pallas_call(hand_on, in_specs=[HBM, HBM], out_specs=(HBM, HBM), out_sh...  2 us

profile of v4, /device:TPU:1, one launch (start us, length us, event | category | flops | bytes accessed | tf_op | source)
XLA Modules:
  0.0 57.3 jit_solution(17192779942369601490)
XLA Ops:
  0.6 54.7 %shard_map.104 = (f32[16,2,64,128]{3,2,1,0:T(8,128)}, f32[1,128]{1,0:T(1,128)}) custom-call(s32[2,128]{1,0:T(2,128)} %ids.1, bf16[128,128,128]{2,1,0:T(8,128)(2,1)} %blocks.1, s32[2,128]{1,0:T(2,128)} %ids.1, s32[1,128]{1,0:T(1,128)} %bitcast.4, s32[1,64]{1,0:T(1,128)} %bitcast.5, s32[1,32]{1,0:T(1,128)} %bitcast.6, f32[8,128]{1,0:T(8,128)} %weight.1, ...), custom_call_target="tpu_custom_call" | custom-call | tf_op jit(solution)/shard_map/pallas_call | solution.py:672
  55.3 2.0 %shard_map.105 = (f32[16,2,64,128]{3,2,1,0:T(8,128)}, f32[1,128]{1,0:T(1,128)}) custom-call(f32[16,2,64,128]{3,2,1,0:T(8,128)} %get-tuple-element.6.coarse_in, f32[1,128]{1,0:T(1,128)} %get-tuple-element.7.relative_in), custom_call_target="tpu_custom_call" | custom-call | tf_op jit(solution)/shard_map/pallas_call | solution.py:737

commit v5 on v4

--- a/solution.py
+++ b/solution.py
@@ -34,10 +34,12 @@
     return lax.dot_general(split, both, NT, preferred_element_type=jnp.float32)
 
 
-def encode(part):
-    peak = jnp.maximum(jnp.max(jnp.abs(part), axis=0, keepdims=True), TINY)
-    code = jnp.round(part * (LEVELS / peak)).astype(jnp.int32)
-    return code.astype(jnp.int16), peak * (1.0 / LEVELS)
+def encode(parts):
+    tops = functools.reduce(jnp.maximum, [jnp.abs(part) for part in parts])
+    peak = jnp.maximum(jnp.max(tops, axis=0, keepdims=True), TINY)
+    up = LEVELS / peak
+    codes = [jnp.round(part * up).astype(jnp.int32).astype(jnp.int16) for part in parts]
+    return codes, peak * (1.0 / LEVELS)
 
 
 def decode(code, scale):
@@ -74,16 +76,22 @@
     n,
     groups,
     across,
-    ids_smem,
     blocks,
-    ids,
-    target_one,
-    target_two,
-    target_three,
-    weight,
-    match_one,
-    match_two,
-    match_three,
+    *rest,
+):
+    given, rest = rest[:8], rest[8:]
+    (coarse, relative), rest = rest[:2], rest[2:]
+    held, rest = rest[:9], rest[9:]
+    body(n, groups, across, blocks, given, held, coarse, relative, *rest)
+
+
+def body(
+    n,
+    groups,
+    across,
+    blocks,
+    given,
+    inputs,
     coarse,
     relative,
     table,
@@ -132,9 +140,11 @@
     three_send,
     three_recv,
     own_sem,
+    input_sem,
     local,
     free,
 ):
+    ids_smem, ids, target_one, target_two, target_three, weight, match_one, match_two, match_three = inputs
     me = lax.axis_index("dev")
     group = lax.axis_index("grp")
     core, chip = me % 2, me // 2
@@ -269,9 +279,6 @@
         other = jnp.where(group < groups // 2, low, high)
         return jnp.where(i == groups - 1, group, other)
 
-    for i in range(trips):
-        own_copy(i).start()
-
     barrier = pltpu.get_barrier_semaphore()
 
     @pl.loop(1, n)
@@ -290,6 +297,14 @@
             barrier, inc=1, device_id={"grp": v, "dev": sibling}, device_id_type=pl.DeviceIdType.MESH
         )
 
+    sources = (given[0], *given)
+    loads = [pltpu.make_async_copy(a, v, input_sem.at[i]) for i, (a, v) in enumerate(zip(sources, inputs))]
+    for load in loads[1:5] + loads[:1] + loads[5:]:
+        load.start()
+    for i in range(trips):
+        own_copy(i).start()
+    for load in loads:
+        load.wait()
     labels[...] = jnp.zeros(labels.shape, jnp.int32)
     labels[0:2, 0:count] = ids[...]
     labels[2:3, 0:count] = target_one[...]
@@ -394,7 +409,7 @@
         parts = []
         for j in range(per_three):
             m = b * per_three + j
-            part = decode(land_half[at, r, m], land_scale_half[at, r, m : m + 1, :])
+            part = decode(land_half[at, r, m], land_scale_half[at, r])
             parts.append(part + from_own(to, b, i, j, core))
         return parts
 
@@ -427,10 +442,9 @@
                 )
 
     def pack(parts, codes, scales):
-        for j, part in enumerate(parts):
-            code, scale = encode(part)
+        packed, scales[...] = encode(parts)
+        for j, code in enumerate(packed):
             codes[j] = code
-            scales[j : j + 1, :] = scale
 
     def start(copies):
         for copy in copies:
@@ -467,7 +481,7 @@
             m = (step - 1) * w + turn
             settle(bulk, one_recv.at[i, b, m])
             parts = [
-                p + decode(land_one[i, b, m, j], land_scale_one[i, b, m, j : j + 1, :])
+                p + decode(land_one[i, b, m, j], land_scale_one[i, b, m])
                 for j, p in enumerate(parts)
             ]
         return parts
@@ -490,7 +504,7 @@
             for turn in range(1, w):
                 settle(bulk, two_recv.at[i, b, turn - 1])
                 parts = [
-                    p + decode(land_two[i, b, turn - 1, j], land_scale_two[i, b, turn - 1, j : j + 1, :])
+                    p + decode(land_two[i, b, turn - 1, j], land_scale_two[i, b, turn - 1])
                     for j, p in enumerate(parts)
                 ]
             pack(parts, out_three.at[i * 2 + b], out_scale_three.at[i * 2 + b])
@@ -568,12 +582,10 @@
 
     third_to_smem.wait()
     end = groups - 1
-    reduced(end)
-    start(send_three(end, 1 - core, group, group, core))
 
     def take(codes, scales, at, h, u):
         for j in range(per_three):
-            part = decode(codes[j], scales[j : j + 1, :])
+            part = decode(codes[j], scales[...])
             sums_three[at + j, h] = part + sums_three[third_smem[0, u * per_three + j], h]
 
     @pl.loop(1, groups)
@@ -582,6 +594,9 @@
         for h in range(2):
             settle(bulk, three_recv.at[u, h])
             take(land_three.at[u, h], land_scale_three.at[u, h], (step - 1) * per_three, h, u)
+
+    reduced(end)
+    start(send_three(end, 1 - core, group, group, core))
 
     take(out_three.at[end * 2 + core], out_scale_three.at[end * 2 + core], end * per_three, core, group)
     other = 1 - core
@@ -626,7 +641,6 @@
         copy.wait()
 
 
-SMEM = pl.BlockSpec(memory_space=pltpu.SMEM)
 VMEM = pl.BlockSpec(memory_space=pltpu.VMEM)
 HBM = pl.BlockSpec(memory_space=pl.ANY)
 VMEM_BYTES = 67_043_328
@@ -666,18 +680,22 @@
     def message(*lead, per=per):
         return [
             pltpu.VMEM(lead + (per, rows, width), jnp.int16),
-            pltpu.VMEM(lead + (per, width), jnp.float32),
+            pltpu.VMEM(lead + (1, width), jnp.float32),
         ] * 2
 
+    targets = [x[None] for x in (target_one, target_two, target_three)]
+    small = [ids_one, *targets, vertex_weights, match_one, match_two, match_three]
     coarse, relative = pl.pallas_call(
         functools.partial(coarsen, n, groups, across),
-        in_specs=[SMEM, HBM] + [VMEM] * 8,
+        in_specs=[HBM] * 9,
         out_specs=(VMEM, VMEM),
         out_shape=(
             jax.ShapeDtypeStruct((count // 8, 2, rows, width), jnp.float32),
             jax.ShapeDtypeStruct((owned // 8, width), jnp.float32),
         ),
         scratch_shapes=[
+            pltpu.SMEM(ids_one.shape, jnp.int32),
+            *[pltpu.VMEM(x.shape, x.dtype) for x in small],
             pltpu.VMEM(match_one.shape, jnp.int32),
             pltpu.VMEM((count, width, width), jnp.bfloat16),
             pltpu.VMEM((ROWS, lanes), jnp.int32),
@@ -698,8 +716,8 @@
             *message(2 * groups)[:2],
             *message(groups, 2)[:2],
             pltpu.VMEM((groups * per + 1, 2, rows, width), jnp.float32),
-            pltpu.VMEM((per * (rows + 2), width), jnp.int16),
-            pltpu.VMEM((2 * per * (rows + 2), width), jnp.int16),
+            pltpu.VMEM((per * rows // 2 + 1, 1, width), jnp.float32),
+            pltpu.VMEM((per * rows + 1, 1, width), jnp.float32),
             pltpu.SemaphoreType.DMA((2,)),
             pltpu.SemaphoreType.DMA((2,)),
             pltpu.SemaphoreType.DMA((2,)),
@@ -713,6 +731,7 @@
             pltpu.SemaphoreType.DMA((2,)),
             pltpu.SemaphoreType.DMA((groups, 2)),
             pltpu.SemaphoreType.DMA((count // math.gcd(count, 16),)),
+            pltpu.SemaphoreType.DMA((9,)),
             pltpu.SemaphoreType.DMA((2,)),
             pltpu.SemaphoreType.REGULAR,
         ],
@@ -722,16 +741,8 @@
             vmem_limit_bytes=VMEM_BYTES,
         ),
     )(
-        ids_one,
         blocks,
-        ids_one,
-        target_one[None],
-        target_two[None],
-        target_three[None],
-        vertex_weights,
-        match_one,
-        match_two,
-        match_three,
+        *small,
     )
     pieces = math.gcd(count // 8, 4)
     coarse, relative = pl.pallas_call(

time: 57.5 us -> 55.8 us (0.970)
  Pallas kernels: 56.7 us -> 55 us
    pallas_call x1, Pallas kernels: 54.7 us -> 53 us  [per_device(): pl.pallas_call(functools.partial(coarsen, n, groups, across), in_specs=[H...]
where the time goes in v5:
time: 55.8 us; the launch traced here: 55.6 us
  Pallas kernels  55 us (99%)
  between operations  0.64 us (1%)
    pallas_call x1, Pallas kernels, per_device(): pl.pallas_call(functools.partial(coarsen, n, groups, across), in_specs=[H...  53 us
    pallas_call x1, Pallas kernels, per_device(): pl.pallas_call(hand_on, in_specs=[HBM, HBM], out_specs=(HBM, HBM), out_sh...  2 us

profile of v5, /device:TPU:1, one launch (start us, length us, event | category | flops | bytes accessed | tf_op | source)
XLA Modules:
  0.0 55.6 jit_solution(6652866758758672414)
XLA Ops:
  0.6 53.0 %shard_map.104 = (f32[16,2,64,128]{3,2,1,0:T(8,128)}, f32[1,128]{1,0:T(1,128)}) custom-call(bf16[128,128,128]{2,1,0:T(8,128)(2,1)} %blocks.1, s32[2,128]{1,0:T(2,128)} %rest_0_.1, s32[1,128]{1,0:T(1,128)} %bitcast.4, s32[1,64]{1,0:T(1,128)} %bitcast.5, s32[1,32]{1,0:T(1,128)} %bitcast.6, f32[8,128]{1,0:T(8,128)} %rest_4_.1, s32[256,128]{1,0:T(8,128)} %rest_5_.1, ...), custom_call_target="tpu_custom_call" | custom-call | tf_op jit(solution)/shard_map/pallas_call | solution.py:688
  53.6 2.0 %shard_map.105 = (f32[16,2,64,128]{3,2,1,0:T(8,128)}, f32[1,128]{1,0:T(1,128)}) custom-call(f32[16,2,64,128]{3,2,1,0:T(8,128)} %get-tuple-element.6.coarse_in, f32[1,128]{1,0:T(1,128)} %get-tuple-element.7.relative_in), custom_call_target="tpu_custom_call" | custom-call | tf_op jit(solution)/shard_map/pallas_call | solution.py:748

commit v6 on v5

--- a/solution.py
+++ b/solution.py
@@ -301,10 +301,11 @@
     loads = [pltpu.make_async_copy(a, v, input_sem.at[i]) for i, (a, v) in enumerate(zip(sources, inputs))]
     for load in loads[1:5] + loads[:1] + loads[5:]:
         load.start()
-    for i in range(trips):
-        own_copy(i).start()
+    own_copy(0).start()
     for load in loads:
         load.wait()
+    for i in range(1, trips):
+        own_copy(i).start()
     labels[...] = jnp.zeros(labels.shape, jnp.int32)
     labels[0:2, 0:count] = ids[...]
     labels[2:3, 0:count] = target_one[...]
@@ -313,17 +314,6 @@
     named = labels[...]
     land_labels[me] = named
     land_far[group] = named
-
-    pl.semaphore_wait(barrier, n - 1 + 2 * (groups - 1))
-
-    @pl.loop(1, n)
-    def _(step):
-        send_labels(peer(step), me).start()
-        send_weight(peer(step), me).start()
-
-    @pl.loop(1, groups)
-    def _(step):
-        send_labels_far(far_peer(step), group).start()
 
     for turn in range(4):
         one = match_one[pl.ds(turn, quarter, stride=4), :]
@@ -348,7 +338,24 @@
             k = i * unroll + j
             sums[k] = parts[j] + sums[plan_smem[0, k] if chained else none]
 
-    @pl.loop(0, max(middle - 1, 0))
+    early = min(2, middle)
+
+    @pl.loop(0, early)
+    def _(i):
+        level(i, False)
+
+    pl.semaphore_wait(barrier, n - 1 + 2 * (groups - 1))
+
+    @pl.loop(1, n)
+    def _(step):
+        send_labels(peer(step), me).start()
+        send_weight(peer(step), me).start()
+
+    @pl.loop(1, groups)
+    def _(step):
+        send_labels_far(far_peer(step), group).start()
+
+    @pl.loop(early, max(middle - 1, early))
     def _(i):
         level(i, False)
 
@@ -382,7 +389,7 @@
     to_smem = pltpu.make_async_copy(plan, plan_smem, local.at[1])
     to_smem.start()
 
-    @pl.loop(max(middle - 1, 0), middle)
+    @pl.loop(max(middle - 1, early), middle)
     def _(i):
         level(i, False)
 

time: 55.8 us -> 55.6 us (level)
  no operation moved by 1% of the time
where the time goes in v6:
time: 55.6 us; the launch traced here: 55.4 us
  Pallas kernels  54.8 us (99%)
  between operations  0.64 us (1%)
    pallas_call x1, Pallas kernels, per_device(): pl.pallas_call(functools.partial(coarsen, n, groups, across), in_specs=[H...  52.8 us
    pallas_call x1, Pallas kernels, per_device(): pl.pallas_call(hand_on, in_specs=[HBM, HBM], out_specs=(HBM, HBM), out_sh...  2 us

profile of v6, /device:TPU:1, one launch (start us, length us, event | category | flops | bytes accessed | tf_op | source)
XLA Modules:
  0.0 55.4 jit_solution(5476021202815430832)
XLA Ops:
  0.6 52.8 %shard_map.104 = (f32[16,2,64,128]{3,2,1,0:T(8,128)}, f32[1,128]{1,0:T(1,128)}) custom-call(bf16[128,128,128]{2,1,0:T(8,128)(2,1)} %blocks.1, s32[2,128]{1,0:T(2,128)} %rest_0_.1, s32[1,128]{1,0:T(1,128)} %bitcast.4, s32[1,64]{1,0:T(1,128)} %bitcast.5, s32[1,32]{1,0:T(1,128)} %bitcast.6, f32[8,128]{1,0:T(8,128)} %rest_4_.1, s32[256,128]{1,0:T(8,128)} %rest_5_.1, ...), custom_call_target="tpu_custom_call" | custom-call | tf_op jit(solution)/shard_map/pallas_call | solution.py:695
  53.4 2.0 %shard_map.105 = (f32[16,2,64,128]{3,2,1,0:T(8,128)}, f32[1,128]{1,0:T(1,128)}) custom-call(f32[16,2,64,128]{3,2,1,0:T(8,128)} %get-tuple-element.6.coarse_in, f32[1,128]{1,0:T(1,128)} %get-tuple-element.7.relative_in), custom_call_target="tpu_custom_call" | custom-call | tf_op jit(solution)/shard_map/pallas_call | solution.py:755
